TPU v7x, 256 devices: a whole 4x4x8 slice. The times are simulated.
256 devices in a mesh: gx: 16 (over y, x), gy: 2 (over core), gz: 8 (over z).
Axes of the slice: x: 4, y: 4, z: 8, core: 2. Of those that a mesh axis runs over, the one named last changes fastest.
Arguments:
- right_side: float32 [81, 64, 16, 1024], P(None, 'gx', 'gy', 'gz'), may hold values from -18 to 18
- cell_coef: float32 [64, 16, 256], P('gx', 'gy', 'gz'), may hold values from 0.5 to 2
- cell_matrix: float32 [81, 81], replicated, may hold values from -2 to 16, as said below
- face_coupling: float32 [3, 81, 81], replicated, may hold values from -0.18 to 0.18
- patch_inverse: bfloat16 [648, 648], replicated, may hold values from -0.01 to 0.1, as said below
Outputs:
- solution: float32 [81, 64, 16, 1024], P(None, 'gx', 'gy', 'gz')
- residual: float32 [81, 64, 16, 1024], P(None, 'gx', 'gy', 'gz')
Inputs may be any that keep to these rules, and one draw needn't show every extreme that they name: `cell_matrix`: symmetric. `patch_inverse`: symmetric.
All inputs are finite; a program needn't handle non-finite values.
Results may differ from a plain program's by a relative error of at most 0.035.
Values may be sent and summed in bfloat16 or wider, within the bound.
A program may use at most 192 MiB of HBM per device.

v0:
```python
import jax
import jax.numpy as jnp
from jax import lax
from jax.sharding import PartitionSpec as P

HIGH = lax.Precision.HIGHEST


def shifted(block, axis, distance):
    devices = range(lax.axis_size(axis))
    route = [((i - distance) % len(devices), i) for i in devices]
    return lax.ppermute(block, axis, route)


def pad_along(values, target, pad_low, pad_high):
    widths = [(0, 0)] * values.ndim
    widths[target] = (pad_low, pad_high)
    return jnp.pad(values, widths)


def cut_along(values, lower_at, upper_at, target):
    return lax.slice_in_dim(values, lower_at, upper_at, axis=target)


def pad_cells(values):
    return jnp.pad(values, ((0, 0), (1, 1), (1, 1), (1, 1), (0, 0)))


def move_x(portion, offset):
    return shifted(portion.astype(jnp.bfloat16), "gx", offset).astype(portion.dtype)


def move_y(portion, offset):
    return shifted(portion.astype(jnp.bfloat16), "gy", offset).astype(portion.dtype)


def move_z(portion, offset):
    return shifted(portion.astype(jnp.bfloat16), "gz", offset).astype(portion.dtype)


def coefficient_frame(cell_coef):
    frame = cell_coef
    arrived = shifted(frame[-1:], "gx", 1)
    frame = jnp.concatenate([arrived, frame], axis=0)
    arrived = shifted(frame[:, -1:], "gy", 1)
    frame = jnp.concatenate([arrived, frame], axis=1)
    arrived = shifted(frame[:, :, -1:], "gz", 1)
    frame = jnp.concatenate([arrived, frame], axis=2)
    return frame


def fetch_lower(scaled, parity):
    region = scaled
    if parity[0] == 0:
        arrived = shifted(region[:, -1:], "gx", 1)
        region = jnp.concatenate([arrived, region[:, :-1]], axis=1)
    if parity[1] == 0:
        arrived = shifted(region[:, :, -1:], "gy", 1)
        region = jnp.concatenate([arrived, region[:, :, :-1]], axis=2)
    if parity[2] == 0:
        arrived = shifted(region[:, :, :, -1:], "gz", 1)
        region = jnp.concatenate([arrived, region[:, :, :, :-1]], axis=3)
    return region


def solve_patches(blocks, region):
    dof_count, extent_x, extent_y, extent_z, rhs_count = region.shape
    blocked = region.reshape(
        dof_count, extent_x // 2, 2, extent_y // 2, 2, extent_z // 2, 2, rhs_count
    )
    solved = jnp.einsum(
        "qijkplmn,pXlYmZnr->qXiYjZkr", blocks, blocked, preferred_element_type=jnp.float32
    )
    return solved.reshape(dof_count, extent_x, extent_y, extent_z, rhs_count)


def fold_changes(correction, parity, coef_frame, cell_matrix, coupling_pairs):
    extent = correction.shape
    coef_region = coef_frame[
        parity[0] : parity[0] + extent[1],
        parity[1] : parity[1] + extent[2],
        parity[2] : parity[2] + extent[3],
    ]
    product = jnp.einsum("pq,qxyzr->pxyzr", cell_matrix, correction, precision=HIGH)
    change = pad_cells(coef_region[None, :, :, :, None] * product)
    for direction in range(3):
        coupled = jnp.einsum(
            "kpq,qxyzr->kpxyzr", coupling_pairs[direction], correction, precision=HIGH
        )
        forward = [(0, 0), (1, 1), (1, 1), (1, 1), (0, 0)]
        backward = list(forward)
        forward[direction + 1] = (0, 2)
        backward[direction + 1] = (2, 0)
        change = change - jnp.pad(coupled[0], forward) - jnp.pad(coupled[1], backward)
    gained = pad_cells(correction)
    senders = (move_x, move_y, move_z)
    for direction in range(3):
        target = direction + 1
        interior = change.shape[target] - 2
        sender = senders[direction]
        if parity[direction] == 0:
            portion = jnp.concatenate(
                [cut_along(change, 0, 2, target), cut_along(gained, 1, 2, target)], axis=target
            )
            arrived = sender(portion, -1)
            change = cut_along(change, 2, interior + 2, target) + pad_along(
                cut_along(arrived, 0, 2, target), target, interior - 2, 0
            )
            gained = cut_along(gained, 2, interior + 2, target) + pad_along(
                cut_along(arrived, 2, 3, target), target, interior - 1, 0
            )
        else:
            from_above = sender(cut_along(change, 0, 1, target), -1)
            from_below = sender(cut_along(change, interior + 1, interior + 2, target), 1)
            change = (
                cut_along(change, 1, interior + 1, target)
                + pad_along(from_above, target, interior - 1, 0)
                + pad_along(from_below, target, 0, interior - 1)
            )
            gained = cut_along(gained, 1, interior + 1, target)
    return (change, gained)


def on_device(right_side, cell_coef, cell_matrix, face_coupling, patch_inverse):
    dof_count = cell_matrix.shape[0]
    extent_x, extent_y, extent_z = cell_coef.shape
    rhs_count = right_side.shape[3] // extent_z
    residual = right_side.reshape(dof_count, extent_x, extent_y, extent_z, rhs_count)
    solution = jnp.zeros_like(residual)
    coef_frame = coefficient_frame(cell_coef)
    scaling_frame = lax.rsqrt(coef_frame)
    scaling_own = scaling_frame[1:, 1:, 1:]
    blocks = patch_inverse.reshape(dof_count, 2, 2, 2, dof_count, 2, 2, 2)
    coupling_pairs = jnp.stack([face_coupling, jnp.swapaxes(face_coupling, 1, 2)], axis=1)
    for colour in range(8):
        parity = (colour // 4, colour // 2 % 2, colour % 2)
        scaled = (scaling_own[None, :, :, :, None] * residual).astype(jnp.bfloat16)
        region = fetch_lower(scaled, parity)
        scaling_region = scaling_frame[
            parity[0] : parity[0] + extent_x,
            parity[1] : parity[1] + extent_y,
            parity[2] : parity[2] + extent_z,
        ]
        correction = scaling_region[None, :, :, :, None] * solve_patches(blocks, region)
        change, gained = fold_changes(correction, parity, coef_frame, cell_matrix, coupling_pairs)
        solution = solution + gained
        residual = residual - change
    return (solution.reshape(right_side.shape), residual.reshape(right_side.shape))


def solution(mesh):
    placed = (P(None, "gx", "gy", "gz"), P("gx", "gy", "gz"), P(), P(), P())
    return jax.shard_map(
        on_device,
        mesh=mesh,
        in_specs=placed,
        out_specs=(P(None, "gx", "gy", "gz"), P(None, "gx", "gy", "gz")),
        check_vma=False,
    )
```

profile of v0, /device:TPU:1, one launch (start us, length us, event | category | flops | bytes accessed | tf_op | source)
XLA Modules:
  0.0 766.3 jit_solution(14943417093921905000)
XLA Ops:
  3.4 4.7 collective-permute-done
  20.7 9.9 %collective-permute-done.3 = bf16[81,1,8,32,4]{0,3,4,2,1:T(8,128)(2,1)S(1)} collective-permute-done((bf16[81,1,8,32,4]{0,3,4,2,1:T(8,128)(2,1)S(1)}, bf16[81,1,8,32,4]{0,3,4,2,1:T(8,128)(2,1)S(1)}, u32[]{:S(2)}, u32[]{:S(2)}) %collective-permute-start.3) | collective-permute-done | bytes 165920 | tf_op jit(solution)/shard_map/ppermute | solution.py:12
  36.2 93.8 %reshape.130 = bf16[81,2,2,2,81,2,2,2]{7,6,5,4,3,2,1,0:T(2,128)(2,1)} reshape(bf16[648,648]{1,0:T(8,128)(2,1)} %param.9) | data formatting | bytes 1679616 | tf_op jit(solution)/shard_map/reshape | solution.py:133
  130.0 109.6 %copy.143 = bf16[81,2,2,2,81,2,2,2,1,1,1]{4,0,7,6,5,3,2,1,10,9,8:T(8,128)(2,1)} copy(bf16[81,2,2,2,81,2,2,2,1,1,1]{7,6,5,4,3,2,1,0,10,9,8:T(2,128)(2,1)} %bitcast.346) | data formatting | bytes 1679616 | tf_op jit(solution)/shard_map/reshape | solution.py:133
  266.1 24.3 %collective-permute-done.6 = bf16[81,3,10,34,4]{0,4,3,2,1:T(4,128)(2,1)S(1)} collective-permute-done((bf16[81,3,10,34,4]{0,4,3,2,1:T(4,128)(2,1)S(1)}, bf16[81,3,10,34,4]{0,4,3,2,1:T(4,128)(2,1)S(1)}, u32[]{:S(2)}, u32[]{:S(2)}) %collective-permute-start.6) | collective-permute-done | bytes 660992 | tf_op jit(solution)/shard_map/ppermute | solution.py:12
  303.9 9.9 %collective-permute-done.9 = bf16[81,1,8,32,4]{0,3,4,2,1:T(8,128)(2,1)S(1)} collective-permute-done((bf16[81,1,8,32,4]{0,3,4,2,1:T(8,128)(2,1)S(1)}, bf16[81,1,8,32,4]{0,3,4,2,1:T(8,128)(2,1)S(1)}, u32[]{:S(2)}, u32[]{:S(2)}) %collective-permute-start.9) | collective-permute-done | bytes 165920 | tf_op jit(solution)/shard_map/ppermute | solution.py:12
  345.1 24.6 %collective-permute-done.11 = bf16[81,3,10,34,4]{0,4,3,2,1:T(4,128)(2,1)S(1)} collective-permute-done((bf16[81,3,10,34,4]{0,4,3,2,1:T(4,128)(2,1)S(1)}, bf16[81,3,10,34,4]{0,4,3,2,1:T(4,128)(2,1)S(1)}, u32[]{:S(2)}, u32[]{:S(2)}) %collective-permute-start.11) | collective-permute-done | bytes 660992 | tf_op jit(solution)/shard_map/ppermute | solution.py:12
  385.8 10.2 %collective-permute-done.15 = bf16[81,1,8,32,4]{0,3,4,2,1:T(8,128)(2,1)S(1)} collective-permute-done((bf16[81,1,8,32,4]{0,3,4,2,1:T(8,128)(2,1)S(1)}, bf16[81,1,8,32,4]{0,3,4,2,1:T(8,128)(2,1)S(1)}, u32[]{:S(2)}, u32[]{:S(2)}) %collective-permute-start.15) | collective-permute-done | bytes 165920 | tf_op jit(solution)/shard_map/ppermute | solution.py:12
  424.0 21.7 %collective-permute-done.17 = bf16[81,3,10,34,4]{0,4,3,2,1:T(4,128)(2,1)S(1)} collective-permute-done((bf16[81,3,10,34,4]{0,4,3,2,1:T(4,128)(2,1)S(1)}, bf16[81,3,10,34,4]{0,4,3,2,1:T(4,128)(2,1)S(1)}, u32[]{:S(2)}, u32[]{:S(2)}) %collective-permute-start.17) | collective-permute-done | bytes 660992 | tf_op jit(solution)/shard_map/ppermute | solution.py:12
  454.0 4.1 collective-permute-done.20
  462.4 8.1 %collective-permute-done.21 = bf16[81,1,8,32,4]{0,3,4,2,1:T(8,128)(2,1)} collective-permute-done((bf16[81,1,8,32,4]{0,3,4,2,1:T(8,128)(2,1)}, bf16[81,1,8,32,4]{0,3,4,2,1:T(8,128)(2,1)}, u32[]{:S(2)}, u32[]{:S(2)}) %collective-permute-start.21) | collective-permute-done | bytes 165920 | tf_op jit(solution)/shard_map/ppermute | solution.py:12
  493.9 22.5 %collective-permute-done.22 = bf16[81,3,10,34,4]{0,4,3,2,1:T(4,128)(2,1)S(1)} collective-permute-done((bf16[81,3,10,34,4]{0,4,3,2,1:T(4,128)(2,1)S(1)}, bf16[81,3,10,34,4]{0,4,3,2,1:T(4,128)(2,1)S(1)}, u32[]{:S(2)}, u32[]{:S(2)}) %collective-permute-start.22) | collective-permute-done | bytes 660992 | tf_op jit(solution)/shard_map/ppermute | solution.py:12
  557.2 4.1 fusion.96
  562.5 4.8 collective-permute-start.29
  567.4 8.5 %collective-permute-done.30 = bf16[81,1,10,34,4]{0,3,4,2,1:T(8,128)(2,1)S(1)} collective-permute-done((bf16[81,1,10,34,4]{0,3,4,2,1:T(8,128)(2,1)S(1)}, bf16[81,1,10,34,4]{0,3,4,2,1:T(8,128)(2,1)S(1)}, u32[]{:S(2)}, u32[]{:S(2)}) %collective-permute-start.30) | collective-permute-done | bytes 220352 | tf_op jit(solution)/shard_map/ppermute | solution.py:12
  609.5 4.1 fusion.95
  614.8 4.9 collective-permute-start.34
  619.8 9.4 %collective-permute-done.35 = bf16[81,1,10,34,4]{0,3,4,2,1:T(8,128)(2,1)S(1)} collective-permute-done((bf16[81,1,10,34,4]{0,3,4,2,1:T(8,128)(2,1)S(1)}, bf16[81,1,10,34,4]{0,3,4,2,1:T(8,128)(2,1)S(1)}, u32[]{:S(2)}, u32[]{:S(2)}) %collective-permute-start.35) | collective-permute-done | bytes 220352 | tf_op jit(solution)/shard_map/ppermute | solution.py:12
  667.5 5.2 fusion.92
  674.0 4.9 collective-permute-start.40
  679.0 6.9 collective-permute-done.41
  721.2 5.2 fusion.89
  727.7 4.9 collective-permute-start.45
  735.6 5.6 collective-permute-done.46
  (472 shorter events, 351.4 us)
Async XLA Ops:
  1.3 6.7 collective-permute-start
  13.1 5.3 collective-permute-start.2
  20.5 10.1 %collective-permute-start.3 = (bf16[81,1,8,32,4]{0,3,4,2,1:T(8,128)(2,1)S(1)}, bf16[81,1,8,32,4]{0,3,4,2,1:T(8,128)(2,1)S(1)}, u32[]{:S(2)}, u32[]{:S(2)}) collective-permute-start(bf16[81,1,8,32,4]{0,3,4,2,1:T(8,128)(2,1)S(1)} %slice.913), channel_id=1, source_target_pairs={{240,0},{0,16},{16,32},{32,48},{48,64},{64,80},{80,96},{96,112},{1... | collective-permute-start | bytes 497672 | tf_op jit(solution)/shard_map/ppermute | solution.py:12
  35.3 207.0 %collective-permute-start.5 = (bf16[81,4,8,1,4]{0,3,4,2,1:T(2,128)(2,1)}, bf16[81,4,8,1,4]{0,3,4,2,1:T(2,128)(2,1)}, u32[]{:S(2)}, u32[]{:S(2)}) collective-permute-start(bf16[81,4,8,1,4]{0,3,4,2,1:T(2,128)(2,1)} %pad_maximum_fusion.25), channel_id=1, source_target_pairs={{7,0},{0,1},{1,2},{2,3},{3,4},{4,5},{5,6},{6,7},{15,8},{8,9},{9,10... | collective-permute-start | bytes 62216 | tf_op jit(solution)/shard_map/ppermute | solution.py:12
  266.0 24.3 %collective-permute-start.6 = (bf16[81,3,10,34,4]{0,4,3,2,1:T(4,128)(2,1)S(1)}, bf16[81,3,10,34,4]{0,4,3,2,1:T(4,128)(2,1)S(1)}, u32[]{:S(2)}, u32[]{:S(2)}) collective-permute-start(bf16[81,3,10,34,4]{0,4,3,2,1:T(4,128)(2,1)S(1)} %copy.94), channel_id=1, source_target_pairs={{16,0},{32,16},{48,32},{64,48},{80,64},{96,80},{112,96},{128,112},... | collective-permute-start | bytes 1982888 | tf_op jit(solution)/shard_map/ppermute | solution.py:12
  303.8 10.0 %collective-permute-start.9 = (bf16[81,1,8,32,4]{0,3,4,2,1:T(8,128)(2,1)S(1)}, bf16[81,1,8,32,4]{0,3,4,2,1:T(8,128)(2,1)S(1)}, u32[]{:S(2)}, u32[]{:S(2)}) collective-permute-start(bf16[81,1,8,32,4]{0,3,4,2,1:T(8,128)(2,1)S(1)} %slice.943), channel_id=1, source_target_pairs={{240,0},{0,16},{16,32},{32,48},{48,64},{64,80},{80,96},{96,112},{1... | collective-permute-start | bytes 497672 | tf_op jit(solution)/shard_map/ppermute | solution.py:12
  315.2 5.8 collective-permute-start.10
  345.0 24.7 %collective-permute-start.11 = (bf16[81,3,10,34,4]{0,4,3,2,1:T(4,128)(2,1)S(1)}, bf16[81,3,10,34,4]{0,4,3,2,1:T(4,128)(2,1)S(1)}, u32[]{:S(2)}, u32[]{:S(2)}) collective-permute-start(bf16[81,3,10,34,4]{0,4,3,2,1:T(4,128)(2,1)S(1)} %copy.102), channel_id=1, source_target_pairs={{16,0},{32,16},{48,32},{64,48},{80,64},{96,80},{112,96},{128,112},... | collective-permute-start | bytes 1982888 | tf_op jit(solution)/shard_map/ppermute | solution.py:12
  376.4 5.6 collective-permute-start.14
  385.7 10.3 %collective-permute-start.15 = (bf16[81,1,8,32,4]{0,3,4,2,1:T(8,128)(2,1)S(1)}, bf16[81,1,8,32,4]{0,3,4,2,1:T(8,128)(2,1)S(1)}, u32[]{:S(2)}, u32[]{:S(2)}) collective-permute-start(bf16[81,1,8,32,4]{0,3,4,2,1:T(8,128)(2,1)S(1)} %slice.968), channel_id=1, source_target_pairs={{240,0},{0,16},{16,32},{32,48},{48,64},{64,80},{80,96},{96,112},{1... | collective-permute-start | bytes 497672 | tf_op jit(solution)/shard_map/ppermute | solution.py:12
  423.9 21.8 %collective-permute-start.17 = (bf16[81,3,10,34,4]{0,4,3,2,1:T(4,128)(2,1)S(1)}, bf16[81,3,10,34,4]{0,4,3,2,1:T(4,128)(2,1)S(1)}, u32[]{:S(2)}, u32[]{:S(2)}) collective-permute-start(bf16[81,3,10,34,4]{0,4,3,2,1:T(4,128)(2,1)S(1)} %copy.109), channel_id=1, source_target_pairs={{16,0},{32,16},{48,32},{64,48},{80,64},{96,80},{112,96},{128,112},... | collective-permute-start | bytes 1982888 | tf_op jit(solution)/shard_map/ppermute | solution.py:12
  459.9 10.6 %collective-permute-start.21 = (bf16[81,1,8,32,4]{0,3,4,2,1:T(8,128)(2,1)}, bf16[81,1,8,32,4]{0,3,4,2,1:T(8,128)(2,1)}, u32[]{:S(2)}, u32[]{:S(2)}) collective-permute-start(bf16[81,1,8,32,4]{0,3,4,2,1:T(8,128)(2,1)} %slice.991), channel_id=1, source_target_pairs={{240,0},{0,16},{16,32},{32,48},{48,64},{64,80},{80,96},{96,112},{1... | collective-permute-start | bytes 497672 | tf_op jit(solution)/shard_map/ppermute | solution.py:12
  493.8 22.6 %collective-permute-start.22 = (bf16[81,3,10,34,4]{0,4,3,2,1:T(4,128)(2,1)S(1)}, bf16[81,3,10,34,4]{0,4,3,2,1:T(4,128)(2,1)S(1)}, u32[]{:S(2)}, u32[]{:S(2)}) collective-permute-start(bf16[81,3,10,34,4]{0,4,3,2,1:T(4,128)(2,1)S(1)} %copy.116), channel_id=1, source_target_pairs={{16,0},{32,16},{48,32},{64,48},{80,64},{96,80},{112,96},{128,112},... | collective-permute-start | bytes 1982888 | tf_op jit(solution)/shard_map/ppermute | solution.py:12
  532.7 5.5 collective-permute-start.28
  562.5 13.5 %collective-permute-start.30 = (bf16[81,1,10,34,4]{0,3,4,2,1:T(8,128)(2,1)S(1)}, bf16[81,1,10,34,4]{0,3,4,2,1:T(8,128)(2,1)S(1)}, u32[]{:S(2)}, u32[]{:S(2)}) collective-permute-start(bf16[81,1,10,34,4]{0,3,4,2,1:T(8,128)(2,1)S(1)} %get-tuple-element.93), channel_id=1, source_target_pairs={{240,0},{0,16},{16,32},{32,48},{48,64},{64,80},{80,96},{96,112},{1... | collective-permute-start | bytes 660968 | tf_op jit(solution)/shard_map/ppermute | solution.py:12
  562.5 13.4 %collective-permute-start.29 = (bf16[81,1,10,34,4]{0,3,4,2,1:T(8,128)(2,1)S(1)}, bf16[81,1,10,34,4]{0,3,4,2,1:T(8,128)(2,1)S(1)}, u32[]{:S(2)}, u32[]{:S(2)}) collective-permute-start(bf16[81,1,10,34,4]{0,3,4,2,1:T(8,128)(2,1)S(1)} %get-tuple-element.92), channel_id=1, source_target_pairs={{16,0},{32,16},{48,32},{64,48},{80,64},{96,80},{112,96},{128,112},... | collective-permute-start | bytes 660968 | tf_op jit(solution)/shard_map/ppermute | solution.py:12
  614.8 14.4 %collective-permute-start.35 = (bf16[81,1,10,34,4]{0,3,4,2,1:T(8,128)(2,1)S(1)}, bf16[81,1,10,34,4]{0,3,4,2,1:T(8,128)(2,1)S(1)}, u32[]{:S(2)}, u32[]{:S(2)}) collective-permute-start(bf16[81,1,10,34,4]{0,3,4,2,1:T(8,128)(2,1)S(1)} %get-tuple-element.91), channel_id=1, source_target_pairs={{240,0},{0,16},{16,32},{32,48},{48,64},{64,80},{80,96},{96,112},{1... | collective-permute-start | bytes 660968 | tf_op jit(solution)/shard_map/ppermute | solution.py:12
  614.8 14.3 %collective-permute-start.34 = (bf16[81,1,10,34,4]{0,3,4,2,1:T(8,128)(2,1)S(1)}, bf16[81,1,10,34,4]{0,3,4,2,1:T(8,128)(2,1)S(1)}, u32[]{:S(2)}, u32[]{:S(2)}) collective-permute-start(bf16[81,1,10,34,4]{0,3,4,2,1:T(8,128)(2,1)S(1)} %get-tuple-element.90), channel_id=1, source_target_pairs={{16,0},{32,16},{48,32},{64,48},{80,64},{96,80},{112,96},{128,112},... | collective-permute-start | bytes 660968 | tf_op jit(solution)/shard_map/ppermute | solution.py:12
  673.9 11.9 %collective-permute-start.41 = (bf16[81,1,10,34,4]{0,3,4,2,1:T(8,128)(2,1)S(1)}, bf16[81,1,10,34,4]{0,3,4,2,1:T(8,128)(2,1)S(1)}, u32[]{:S(2)}, u32[]{:S(2)}) collective-permute-start(bf16[81,1,10,34,4]{0,3,4,2,1:T(8,128)(2,1)S(1)} %get-tuple-element.89), channel_id=1, source_target_pairs={{240,0},{0,16},{16,32},{32,48},{48,64},{64,80},{80,96},{96,112},{1... | collective-permute-start | bytes 660968 | tf_op jit(solution)/shard_map/ppermute | solution.py:12
  674.0 11.8 %collective-permute-start.40 = (bf16[81,1,10,34,4]{0,3,4,2,1:T(8,128)(2,1)S(1)}, bf16[81,1,10,34,4]{0,3,4,2,1:T(8,128)(2,1)S(1)}, u32[]{:S(2)}, u32[]{:S(2)}) collective-permute-start(bf16[81,1,10,34,4]{0,3,4,2,1:T(8,128)(2,1)S(1)} %get-tuple-element.88), channel_id=1, source_target_pairs={{16,0},{32,16},{48,32},{64,48},{80,64},{96,80},{112,96},{128,112},... | collective-permute-start | bytes 660968 | tf_op jit(solution)/shard_map/ppermute | solution.py:12
  727.7 13.5 %collective-permute-start.46 = (bf16[81,1,10,34,4]{0,3,4,2,1:T(8,128)(2,1)S(1)}, bf16[81,1,10,34,4]{0,3,4,2,1:T(8,128)(2,1)S(1)}, u32[]{:S(2)}, u32[]{:S(2)}) collective-permute-start(bf16[81,1,10,34,4]{0,3,4,2,1:T(8,128)(2,1)S(1)} %get-tuple-element.87), channel_id=1, source_target_pairs={{240,0},{0,16},{16,32},{32,48},{48,64},{64,80},{80,96},{96,112},{1... | collective-permute-start | bytes 660968 | tf_op jit(solution)/shard_map/ppermute | solution.py:12
  727.7 13.4 %collective-permute-start.45 = (bf16[81,1,10,34,4]{0,3,4,2,1:T(8,128)(2,1)S(1)}, bf16[81,1,10,34,4]{0,3,4,2,1:T(8,128)(2,1)S(1)}, u32[]{:S(2)}, u32[]{:S(2)}) collective-permute-start(bf16[81,1,10,34,4]{0,3,4,2,1:T(8,128)(2,1)S(1)} %get-tuple-element.86), channel_id=1, source_target_pairs={{16,0},{32,16},{48,32},{64,48},{80,64},{96,80},{112,96},{128,112},... | collective-permute-start | bytes 660968 | tf_op jit(solution)/shard_map/ppermute | solution.py:12
  747.4 12.1 %collective-permute-start.50 = (bf16[81,4,8,1,4]{0,3,4,2,1:T(2,128)(2,1)S(1)}, bf16[81,4,8,1,4]{0,3,4,2,1:T(2,128)(2,1)S(1)}, u32[]{:S(2)}, u32[]{:S(2)}) collective-permute-start(bf16[81,4,8,1,4]{0,3,4,2,1:T(2,128)(2,1)S(1)} %get-tuple-element.103), channel_id=1, source_target_pairs={{7,0},{0,1},{1,2},{2,3},{3,4},{4,5},{5,6},{6,7},{15,8},{8,9},{9,10... | collective-permute-start | bytes 62216 | tf_op jit(solution)/shard_map/ppermute | solution.py:12
  748.0 11.5 %collective-permute-start.49 = (bf16[81,4,8,1,4]{0,3,4,2,1:T(2,128)(2,1)S(1)}, bf16[81,4,8,1,4]{0,3,4,2,1:T(2,128)(2,1)S(1)}, u32[]{:S(2)}, u32[]{:S(2)}) collective-permute-start(bf16[81,4,8,1,4]{0,3,4,2,1:T(2,128)(2,1)S(1)} %get-tuple-element.102), channel_id=1, source_target_pairs={{1,0},{2,1},{3,2},{4,3},{5,4},{6,5},{7,6},{0,7},{9,8},{10,9},{11,1... | collective-permute-start | bytes 62216 | tf_op jit(solution)/shard_map/ppermute | solution.py:12
  (92 other events, 607.2 us)
where the time goes:
time: 777 us; the launch traced here: 766 us
  local copies, waits for them, and re-layouts  287 us (37%)
  waiting for transfers between devices  209 us (27%)
  matrix products  113 us (15%)
  other arithmetic  79.1 us (10%)
  starting transfers between devices  75.8 us (10%)
    ppermute x51, waiting for transfers between devices, shifted(): return lax.ppermute(block, axis, route)  209 us
    reshape x2, local copies, waits for them, and re-layouts, on_device(): blocks = patch_inverse.reshape(dof_count, 2, 2, 2, dof_count, 2, 2, 2)  203 us
    dot_general x24, matrix products, fold_changes(): jnp.einsum('kpq,qxyzr->kpxyzr', coupling_pairs[direction], correction, pr...  87.3 us
    ppermute x51, starting transfers between devices, shifted(): return lax.ppermute(block, axis, route)  75.8 us
    another operation x12, other arithmetic  24.2 us
    unnamed x129, local copies, waits for them, and re-layouts  22.6 us
    mul x22, local copies, waits for them, and re-layouts, on_device(): scaling_region[None, :, :, :, None] * solve_patches(blocks, region)  18.1 us
    squeeze x24, local copies, waits for them, and re-layouts, fold_changes(): coupled[0]  15.7 us
  transfers between devices with their start and end apart: 51, of which 40 were waited for; matrix products, arithmetic and copies ran while one was open for 30% of the time, Pallas kernels for 0%

commit v1 on v0

v1 whole, which is shorter than its diff:
```python
import functools

import jax
import jax.numpy as jnp
from jax import lax
from jax.experimental import pallas as pl
from jax.experimental.pallas import tpu as pltpu
from jax.sharding import PartitionSpec as P

Q = 81
F = 88
B = 96
L = 128
F32, BF16 = jnp.float32, jnp.bfloat16

SWAP, SINIT, SHIFT, PRE, POSTX, POSTZ, MID, OUTS, COPIES = 0, 1, 3, 5, 9, 17, 21, 23, 25


def padded(tile):
    return jnp.concatenate([tile, jnp.zeros((B - F, tile.shape[1]), F32)], axis=0).astype(BF16)


def roll(tile, shift):
    shift = shift % L
    return pltpu.roll(tile, shift, 1) if shift else tile


def kernel(
    nx, nz,
    b_ref, coef_ref, p_ref, w_ref,
    sol_ref, res_ref,
    perm, perm_back, stage, arrive, partner_in, R, S, SN, CF, SEP, SOM, su, sd, hsl, hsu,
    xs, xr, XK, OUT, CB, DB, YR, ZR, XL, XU, PU, PD, HL, HU, QU, QD, GL, GU, MS, MR, OIN, OS,
    send_sem, recv_sem,
):
    gx, gy, gz = lax.axis_index("gx"), lax.axis_index("gy"), lax.axis_index("gz")
    partner = (gx, 1 - gy, gz)
    x_up, x_down = (lax.rem(gx + 1, nx), gy, gz), (lax.rem(gx + nx - 1, nx), gy, gz)
    z_up, z_down = (gx, gy, lax.rem(gz + 1, nz)), (gx, gy, lax.rem(gz + nz - 1, nz))

    def copy(index, src, dst, device):
        return pltpu.make_async_remote_copy(
            src_ref=src, dst_ref=dst, send_sem=send_sem.at[index], recv_sem=recv_sem.at[index],
            device_id=device, device_id_type=pl.DeviceIdType.MESH,
        )

    barrier = pltpu.get_barrier_semaphore()
    for device in (partner, x_up, x_down, z_up, z_down):
        pl.semaphore_signal(barrier, inc=1, device_id=device, device_id_type=pl.DeviceIdType.MESH)

    lane = lax.broadcasted_iota(jnp.int32, (F, L), 1)
    zlane = lax.rem(lane, 16)
    first, last = zlane == 0, zlane == 15
    lane96 = lax.broadcasted_iota(jnp.int32, (B, L), 1)
    half96 = lane96 < 64
    lane8 = lax.broadcasted_iota(jnp.int32, (8, L), 1)
    zlane8 = lax.rem(lane8, 16)

    def source_of(n):
        r, zp, y, zq = n // 128, (n // 64) % 2, (n // 16) % 4, n % 16
        return y * 128 + (2 * zq + zp) * 4 + r

    rows = lax.broadcasted_iota(jnp.int32, (128, 512), 0)
    cols = lax.broadcasted_iota(jnp.int32, (128, 512), 1)
    for i in range(4):
        perm[128 * i : 128 * i + 128, :] = (rows + 128 * i == source_of(cols)).astype(F32).astype(BF16)
        perm_back[128 * i : 128 * i + 128, :] = (source_of(rows + 128 * i) == cols).astype(F32).astype(BF16)

    stage[...] = jnp.zeros_like(stage)
    S[...] = jnp.zeros_like(S)

    def enter(x, carry):
        for yp in range(2):
            for y in range(4):
                row = x * 8 + 2 * y + yp
                stage[0:Q, y * L : y * L + L] = b_ref[pl.ds(row, Q, 32), :]
                coef = coef_ref[pl.ds(row, 1), :]
                high = coef.astype(BF16).astype(F32)
                stage[Q : Q + 1, y * L : y * L + L] = high
                stage[Q + 1 : Q + 2, y * L : y * L + L] = coef - high
            sorted_ = jnp.dot(stage[...].astype(BF16), perm[...], preferred_element_type=F32)
            for r in range(4):
                arrive[r, x, yp] = sorted_[:, r * L : r * L + L].astype(BF16)
        return carry

    lax.fori_loop(0, 4, enter, 0)
    pl.semaphore_wait(barrier, 5)
    swap = copy(SWAP, arrive.at[pl.ds(2 * (1 - gy), 2)], partner_in, partner)
    swap.start()
    swap.wait()

    def gather(h, x, yp):
        own = arrive[2 * gy + h, x, yp].astype(F32)
        other = partner_in[h, x, yp].astype(F32)
        lo, hi = jnp.where(gy == 0, own, other), jnp.where(gy == 0, other, own)
        return jnp.where(half96, lo, roll(hi, 64)), jnp.where(half96, roll(lo, 64), hi)

    def keep_coef(xi, yp, zp, tile):
        coef = jnp.broadcast_to(tile[Q : Q + 1] + tile[Q + 1 : Q + 2], (8, L))
        CF[xi, yp, zp] = coef
        SN[xi, yp, zp] = lax.rsqrt(coef)

    shifts = [copy(SHIFT + h, xs.at[h], xr.at[h], x_up) for h in range(2)]
    for h in range(2):
        for yp in range(2):
            for zp, tile in enumerate(gather(h, 3, yp)):
                xs[h, yp, zp] = tile.astype(BF16)
                if h == 0:
                    keep_coef(4, yp, zp, tile)
        shifts[h].start()

    def place(x, carry):
        for h in range(2):
            for yp in range(2):
                for zp, tile in enumerate(gather(h, x, yp)):
                    R[h, x, yp, zp] = tile[:F]
                    if h == 0:
                        keep_coef(x + 1, yp, zp, tile)
        return carry

    lax.fori_loop(0, 3, place, 0)
    for h in range(2):
        shifts[h].wait()
        for yp in range(2):
            for zp in range(2):
                tile = xr[h, yp, zp].astype(F32)
                R[h, 3, yp, zp] = tile[:F]
                if h == 0:
                    keep_coef(0, yp, zp, tile)

    up, down = jnp.zeros((8, L), F32), jnp.zeros((8, L), F32)
    for xi in range(5):
        for yp in range(2):
            j = 2 * xi + yp
            up = jnp.where(zlane8 == j, roll(SN[xi, yp, 1], j - 15), up)
            down = jnp.where(zlane8 == j, roll(SN[xi, yp, 0], j), down)
    su[...] = up
    sd[...] = down
    s_copies = [copy(SINIT, su, hsl, z_up), copy(SINIT + 1, sd, hsu, z_down)]
    for c in s_copies:
        c.start()
    for c in s_copies:
        c.wait()
    for xi in range(5):
        for yp in range(2):
            j = 2 * xi + yp
            SEP[xi, yp] = jnp.where(zlane8 == 15, roll(hsu[...], 15 - j), roll(SN[xi, yp, 0], -1))
            SOM[xi, yp] = jnp.where(zlane8 == 0, roll(hsl[...], -j), roll(SN[xi, yp, 1], 1))

    def round_of_four(a, carry):
        def slot(l):
            return lax.rem(l + 3 * (1 - a), 4)

        def times(ref, index, tile):
            return ref[index][0:1] * tile

        mids = [copy(MID + h, MS.at[h], MR.at[h], x_down) for h in range(2)]

        @pl.when(a == 1)
        def _():
            for h in range(2):
                for yp in range(2):
                    for zp in range(2):
                        MS[h, 0, yp, zp] = padded(R[h, 3, yp, zp])
                        MS[h, 1, yp, zp] = padded(S[h, 3, yp, zp])
                mids[h].start()
            for h in range(2):
                mids[h].wait()
                for yp in range(2):
                    for zp in range(2):
                        R[h, 3, yp, zp] = MR[h, 0, yp, zp][:F].astype(F32)
                        S[h, 3, yp, zp] = MR[h, 1, yp, zp][:F].astype(F32)

        def pre_copies(h):
            return (
                copy(PRE + 2 * h, PU.at[h], HL.at[h], z_up),
                copy(PRE + 2 * h + 1, PD.at[h], HU.at[h], z_down),
            )

        def x_copies(h, g):
            return (
                copy(POSTX + 4 * h + 2 * g, CB.at[h, slot(3)], XL.at[h, g], x_up),
                copy(POSTX + 4 * h + 2 * g + 1, CB.at[h, slot(0)], XU.at[h, g], x_down),
            )

        def z_copies(h):
            return (
                copy(POSTZ + 2 * h, QU.at[h], GL.at[h], z_up),
                copy(POSTZ + 2 * h + 1, QD.at[h], GU.at[h], z_down),
            )

        def pre(h):
            up, down = jnp.zeros((F, L), F32), jnp.zeros((F, L), F32)
            for l in range(4):
                for yp in range(2):
                    j = 2 * l + yp
                    tile = times(SN, (l + a, yp, 1), R[h, slot(l), yp, 1])
                    up = jnp.where(zlane == j, roll(tile, j - 15), up)
                    tile = times(SN, (l + a, yp, 0), R[h, slot(l), yp, 0])
                    down = jnp.where(zlane == j, roll(tile, j), down)
            PU[h] = padded(up)
            PD[h] = padded(down)
            for c in pre_copies(h):
                c.start()

        def frames(b, g):
            for dx in range(2):
                for dy in range(2):
                    for dz in range(2):
                        yp, zp = (dy if b else 1 - dy), (dz if g else 1 - dz)
                        ry, rz = int(not b and dy == 0), int(not g and dz == 0)
                        yield 4 * dx + 2 * dy + dz, dx, yp, zp, ry, rz

        def solve(h, b, g):
            if g == 0:
                for c in pre_copies(h):
                    c.wait_recv()
            for k, dx, yp, zp, ry, rz in frames(b, g):
                for X in range(2):
                    l = 2 * X + dx
                    tile = times(SN, (l + a, yp, zp), R[h, slot(l), yp, zp])
                    tile = roll(tile, 16 * ry + rz)
                    if rz:
                        ghost = roll(HL[h].astype(F32)[:F], 16 * ry - (2 * l + yp))
                        tile = jnp.where(first, ghost, tile)
                    XK[k * B : k * B + B, X * L : X * L + L] = padded(tile)
                if g == 0:
                    edge = (PU if rz else HU)[h].astype(F32)
                    XK[k * B : k * B + B, 2 * L : 3 * L] = roll(edge, 16 * ry - (2 * dx + yp)).astype(BF16)
            width = 256 if g else 384
            OUT[:, :width] = jnp.dot(p_ref[...], XK[:, :width], preferred_element_type=F32)
            if g == 0:
                for c in pre_copies(h):
                    c.wait_send()
            up, down = jnp.zeros((F, L), F32), jnp.zeros((F, L), F32)
            for X in range(2):
                for k, dx, yp, zp, ry, rz in frames(b, g):
                    l = 2 * X + dx
                    j = 2 * l + yp
                    block = OUT[k * F : k * F + F, X * L : X * L + L]
                    if g:
                        corr = times(SN, (l + a, yp, zp), roll(block, -16 * ry))
                        if zp:
                            up = jnp.where(zlane == j, roll(corr, j - 15), up)
                            beside = roll(corr, 1)
                        else:
                            down = jnp.where(zlane == j, roll(corr, j), down)
                            beside = roll(corr, -1)
                    else:
                        edge = OUT[k * F : k * F + F, 2 * L : 3 * L]
                        here = roll(block, -16 * ry)
                        above = jnp.where(last, roll(edge, 15 - 4 * X - 16 * ry), roll(block, -16 * ry - 1))
                        if zp:
                            corr = times(SN, (l + a, yp, 1), above)
                            beside = times(SOM, (l + a, yp), here)
                        else:
                            corr = times(SN, (l + a, yp, 0), here)
                            beside = times(SEP, (l + a, yp), above)
                    S[h, slot(l), yp, zp] += corr
                    CB[h, slot(l), yp, zp] = padded(corr)
                    DB[h, slot(l), yp, zp] = padded(times(CF, (l + a, yp, zp), corr))
                    YR[h, slot(l), yp, zp] = padded(roll(corr, 16 if yp else -16))
                    ZR[h, slot(l), yp, zp] = padded(beside)
                x_copies(h, g)[1 - X].start()
            if g:
                QU[h] = padded(up)
                QD[h] = padded(down)
                for c in z_copies(h):
                    c.start()

        def update(h, g):
            if g:
                for c in z_copies(h):
                    c.wait_recv()
            for l in (1, 2, 0, 3):
                if l == 0:
                    x_copies(h, g)[0].wait_recv()
                if l == 3:
                    x_copies(h, g)[1].wait_recv()
                for yp in range(2):
                    s = slot(l)
                    j = 2 * l + yp
                    pair = lambda ref, *index: [ref[(*index, 0)], ref[(*index, 1)]]
                    own = pair(CB, h, s, yp)
                    behind, ahead = ZR[h, s, yp, 1], ZR[h, s, yp, 0]
                    if g:
                        ghost = roll(GL[h].astype(F32)[:F], -j)
                        behind = padded(jnp.where(first, ghost, behind.astype(F32)[:F]))
                        ghost = roll(GU[h].astype(F32)[:F], 15 - j)
                        ahead = padded(jnp.where(last, ghost, ahead.astype(F32)[:F]))
                    blocks = [
                        pair(DB, h, s, yp),
                        pair(CB, h, slot(l - 1), yp) if l else pair(XL, h, g, yp),
                        pair(CB, h, slot(l + 1), yp) if l < 3 else pair(XU, h, g, yp),
                        pair(CB, h, s, 0) if yp else pair(YR, h, s, 1),
                        pair(YR, h, s, 0) if yp else pair(CB, h, s, 1),
                        [behind, own[0]],
                        [own[1], ahead],
                    ]
                    stacked = jnp.concatenate([jnp.concatenate(block, axis=1) for block in blocks], axis=0)
                    change = jnp.dot(w_ref[...], stacked, preferred_element_type=F32)
                    R[h, s, yp, 0] -= change[:, :L]
                    R[h, s, yp, 1] -= change[:, L:]
            for c in x_copies(h, g) + (z_copies(h) if g else ()):
                c.wait_send()

        for h in range(2):
            pre(h)
        for b in range(2):
            for g in range(2):
                for h in range(2):
                    solve(h, b, g)
                for h in range(2):
                    update(h, g)
                    if g == 1 and b == 0:
                        pre(h)
        return carry

    lax.fori_loop(0, 2, round_of_four, 0)

    outs = [copy(OUTS + w, OS.at[w], OIN.at[w, pl.ds(2 * gy, 2)], partner) for w in range(2)]
    for w, field in enumerate((S, R)):

        def leave(x, carry):
            for h in range(2):
                for yp in range(2):
                    even, odd = field[h, x, yp, 0], field[h, x, yp, 1]
                    lo = jnp.where(lane < 64, even, roll(odd, 64))
                    hi = jnp.where(lane < 64, roll(even, 64), odd)
                    OIN[w, 2 * gy + h, x, yp] = padded(jnp.where(gy == 0, lo, hi))
                    OS[w, h, x, yp] = padded(jnp.where(gy == 0, hi, lo))
            return carry

        lax.fori_loop(0, 4, leave, 0)
        outs[w].start()
    for w, out_ref in enumerate((sol_ref, res_ref)):
        outs[w].wait()

        def finish(x, carry):
            for yp in range(2):
                tiles = jnp.concatenate([OIN[w, r, x, yp] for r in range(4)], axis=1)
                back = jnp.dot(tiles, perm_back[...], preferred_element_type=F32)
                for y in range(4):
                    out_ref[pl.ds(x * 8 + 2 * y + yp, Q, 32), :] = back[:Q, y * L : y * L + L]
            return carry

        lax.fori_loop(0, 4, finish, 0)


def on_device(nx, nz, right_side, cell_coef, cell_matrix, face_coupling, patch_inverse):
    flat = right_side.reshape(-1, L)
    coef = jnp.repeat(cell_coef, 4, axis=2).reshape(-1, L)
    blocks = patch_inverse.reshape(Q, 8, Q, 8).transpose(1, 0, 3, 2)
    blocks = jnp.pad(blocks, ((0, 0), (0, F - Q), (0, 0), (0, B - Q))).reshape(8 * F, 8 * B)
    parts = [cell_matrix]
    for d in range(3):
        parts += [-face_coupling[d].T, -face_coupling[d]]
    weights = jnp.concatenate([jnp.pad(p, ((0, F - Q), (0, B - Q))) for p in parts], axis=1).astype(BF16)
    tile = lambda *dims, t=BF16: pltpu.VMEM((*dims, B if t == BF16 else F, L), t)
    vmem = pl.BlockSpec(memory_space=pltpu.VMEM)
    sol, res = pl.pallas_call(
        functools.partial(kernel, nx, nz),
        out_shape=[jax.ShapeDtypeStruct(flat.shape, F32)] * 2,
        in_specs=[vmem] * 4,
        out_specs=[vmem] * 2,
        scratch_shapes=[
            pltpu.VMEM((512, 512), BF16),
            pltpu.VMEM((512, 512), BF16),
            pltpu.VMEM((B, 512), F32),
            tile(4, 4, 2),
            tile(2, 4, 2),
            tile(2, 4, 2, 2, t=F32),
            tile(2, 4, 2, 2, t=F32),
            pltpu.VMEM((5, 2, 2, 8, L), F32),
            pltpu.VMEM((5, 2, 2, 8, L), F32),
            pltpu.VMEM((5, 2, 8, L), F32),
            pltpu.VMEM((5, 2, 8, L), F32),
            *[pltpu.VMEM((8, L), F32)] * 4,
            tile(2, 2, 2), tile(2, 2, 2),
            pltpu.VMEM((8 * B, 3 * L), BF16),
            pltpu.VMEM((8 * F, 3 * L), F32),
            *[tile(2, 4, 2, 2)] * 4,
            *[tile(2, 2, 2, 2)] * 2,
            *[tile(2)] * 8,
            *[tile(2, 2, 2, 2)] * 2,
            tile(2, 4, 4, 2),
            tile(2, 2, 4, 2),
            pltpu.SemaphoreType.DMA((COPIES,)),
            pltpu.SemaphoreType.DMA((COPIES,)),
        ],
        compiler_params=pltpu.CompilerParams(
            collective_id=0, has_side_effects=True, vmem_limit_bytes=60 * 1024 * 1024
        ),
    )(flat, coef, blocks, weights)
    return sol.reshape(right_side.shape), res.reshape(right_side.shape)


def solution(mesh):
    fields = P(None, "gx", "gy", "gz")
    return jax.shard_map(
        functools.partial(on_device, mesh.shape["gx"], mesh.shape["gz"]),
        mesh=mesh,
        in_specs=(fields, P("gx", "gy", "gz"), P(), P(), P()),
        out_specs=(fields, fields),
        check_vma=False,
    )
```

time: 777 us -> 156 us (0.20); the launches traced: 766 us -> 155 us
  local copies, waits for them, and re-layouts: 287 us -> 34.1 us
  waiting for transfers between devices: 209 us -> 0 us
  Pallas kernels: 0 us -> 121 us
  matrix products: 113 us -> 0 us
  other arithmetic: 79.1 us -> 0.03 us
  starting transfers between devices: 75.8 us -> 0 us
    ppermute x51 -> x0, waiting for transfers between devices: 209 us -> none  [shifted(): return lax.ppermute(block, axis, route)]
    reshape x2, local copies, waits for them, and re-layouts: 203 us -> 15.9 us  [the longest x1 13.8 us: on_device(): blocks = patch_inverse.reshape(Q, 8, Q, 8).transpose(1, 0, 3, 2)]
    pallas_call x0 -> x1, Pallas kernels: none -> 121 us  [on_device(): pl.pallas_call(functools.partial(kernel, nx, nz), out_shape=[jax.ShapeDty...]
    dot_general x40 -> x0, matrix products: 113 us -> none  [the longest x24 87.3 us: fold_changes(): jnp.einsum('kpq,qxyzr->kpxyzr', coupling_pairs[direction], correction, pr...]
    ppermute x51 -> x0, starting transfers between devices: 75.8 us -> none  [shifted(): return lax.ppermute(block, axis, route)]
    another operation x12 -> x1, other arithmetic: 24.2 us -> 0.01 us
    mul x24 -> x0, local copies, waits for them, and re-layouts: 18.5 us -> none  [the longest x22 18.1 us: on_device(): scaling_region[None, :, :, :, None] * solve_patches(blocks, region)]
    convert_element_type x12 -> x0, other arithmetic: 16.5 us -> none  [the longest x8 15.4 us: on_device(): scaled = (scaling_own[None, :, :, :, None] * residual).astype(jnp.bfloat16)]
  transfers between devices with their start and end apart: 51 -> 0, of which waited for: 40 -> 0; matrix products, arithmetic and copies ran while one was open for 30% -> 0% of each run, Pallas kernels for 0% -> 0%
where the time goes in v1:
time: 156 us; the launch traced here: 155 us
  Pallas kernels  121 us (78%)
  local copies, waits for them, and re-layouts  34.1 us (22%)
    pallas_call x1, Pallas kernels, on_device(): pl.pallas_call(functools.partial(kernel, nx, nz), out_shape=[jax.ShapeDty...  121 us
    unnamed x13, local copies, waits for them, and re-layouts  16.1 us
    reshape x1, local copies, waits for them, and re-layouts, on_device(): blocks = patch_inverse.reshape(Q, 8, Q, 8).transpose(1, 0, 3, 2)  13.8 us

profile of v1, /device:TPU:1, one launch (start us, length us, event | category | flops | bytes accessed | tf_op | source)
XLA Modules:
  0.0 155.4 jit_solution(6231520584677136422)
XLA Ops:
  0.6 0.8 copy.11
  1.5 0.2 reshape_reshape.3
  1.6 0.7 copy.16.coef_ref
  2.3 13.8 %reshape.32 = bf16[81,8,81,8]{3,2,1,0:T(8,128)(2,1)} reshape(bf16[648,648]{1,0:T(8,128)(2,1)} %param.9) | data formatting | bytes 1679616 | tf_op jit(solution)/shard_map/reshape | solution.py:353
  16.2 11.3 %copy.17 = bf16[8,81,8,81]{3,2,1,0:T(8,128)(2,1)S(1)} copy(bf16[8,81,8,81]{2,3,0,1:T(8,128)(2,1)} %bitcast.23) | data formatting | bytes 1679616
  27.5 0.3 pad.33.clone
  27.8 0.0 copy-start.2
  27.8 0.0 copy-start.1
  27.8 2.0 %reshape.33.p_ref = bf16[704,768]{1,0:T(8,128)(2,1)} reshape(bf16[8,88,8,96]{3,2,1,0:T(8,128)(2,1)S(1)} %pad.33.clone) | data formatting | bytes 2162688 | tf_op jit(solution)/shard_map/reshape | solution.py:354
  29.9 0.0 copy-done.2
  29.9 0.0 copy-done.1
  29.9 0.1 copy.18
  30.1 0.1 copy.19
  30.2 0.1 copy.20
  30.4 0.8 concatenate.4.w_ref
  31.2 120.5 %shard_map.68 = (f32[2592,128]{1,0:T(8,128)}, f32[2592,128]{1,0:T(8,128)}) custom-call(f32[2592,128]{1,0:T(8,128)} %bitcast.24, f32[32,128]{1,0:T(8,128)} %copy.16.coef_ref, bf16[704,768]{1,0:T(8,128)(2,1)} %reshape.33.p_ref, bf16[88,672]{1,0:T(8,128)(2,1)} %concatenate.4.w_ref), custom_call_target="tpu_custom_call" | custom-call | tf_op jit(solution)/shard_map/pallas_call | solution.py:361
  151.7 0.0 copy-start
  151.7 2.6 %copy.23 = f32[81,4,8,128]{3,2,1,0:T(8,128)} copy(f32[81,4,8,128]{3,2,1,0:T(8,128)} %bitcast.26) | data formatting | bytes 2654208
  154.3 0.0 copy-done
  154.3 1.1 copy.24
  (10 shorter events, 0.2 us)
Async XLA Ops:
  27.8 2.0 %copy-start.2 = (f32[81,81]{1,0:T(8,128)S(1)}, f32[81,81]{1,0:T(8,128)}, u32[]{:S(2)}) copy-start(f32[81,81]{1,0:T(8,128)} %param.7) | copy-start | bytes 78736
  27.8 2.1 %copy-start.1 = (f32[3,81,81]{2,1,0:T(8,128)S(1)}, f32[3,81,81]{2,1,0:T(8,128)}, u32[]{:S(2)}) copy-start(f32[3,81,81]{2,1,0:T(8,128)} %param.8) | copy-start | bytes 236200
  151.7 2.6 %copy-start = (f32[2592,128]{1,0:T(8,128)S(1)}, f32[2592,128]{1,0:T(8,128)}, u32[]{:S(2)}) copy-start(f32[2592,128]{1,0:T(8,128)} %get-tuple-element.5) | copy-start | bytes 3981316

commit v2 on v1

v2 whole, which is shorter than its diff:
```python
import functools

import jax
import jax.numpy as jnp
from jax import lax
from jax.experimental import pallas as pl
from jax.experimental.pallas import tpu as pltpu
from jax.sharding import PartitionSpec as P

Q = 81
F = 88
B = 96
L = 128
F32, BF16 = jnp.float32, jnp.bfloat16
MESH = pl.DeviceIdType.MESH

SWAP, SINIT, SHIFT, PRE, POSTX, POSTZ, MID, OUTS, COPIES = 0, 1, 3, 5, 9, 17, 21, 25, 29


def padded(tile):
    return jnp.concatenate([tile, jnp.zeros((B - F, tile.shape[1]), F32)], axis=0).astype(BF16)


def roll(tile, shift):
    shift = shift % L
    return pltpu.roll(tile, shift, 1) if shift else tile


def one_hot(shape, hit):
    rows = lax.broadcasted_iota(jnp.int32, shape, 0)
    cols = lax.broadcasted_iota(jnp.int32, shape, 1)
    return jnp.where(hit(rows, cols), 1.0, 0.0).astype(BF16)


def source_of(n):
    return ((n >> 4) & 3) * 128 + (n & 15) * 8 + ((n >> 6) & 1) * 4 + (n >> 7)


def kernel(
    nx, nz,
    b_ref, coef_ref, p_ref, m_ref, f_ref,
    out_ref,
    perm, stage, coefs, p_rows, p_cols, p_stack, PINV, square, W,
    arrive, partner_in, R, S, SN, CF, SEP, SOM, su, sd, hsl, hsu,
    xr, XK, OUT, CB, DB, YR, ZR, XL, XU, PU, PD, HL, HU, QU, QD, GL, GU, MS, MR, OIN, OS,
    send_sem, recv_sem, out_sem,
):
    gx, gy, gz = lax.axis_index("gx"), lax.axis_index("gy"), lax.axis_index("gz")
    up_x, down_x = lax.rem(gx + 1, nx), lax.rem(gx + nx - 1, nx)
    partner = (gx, 1 - gy, gz)
    x_up, x_down = (up_x, gy, gz), (down_x, gy, gz)
    z_up, z_down = (gx, gy, lax.rem(gz + 1, nz)), (gx, gy, lax.rem(gz + nz - 1, nz))
    cross_up, cross_down = (up_x, 1 - gy, gz), (down_x, 1 - gy, gz)

    def copy(index, src, dst, device):
        return pltpu.make_async_remote_copy(
            src_ref=src, dst_ref=dst, send_sem=send_sem.at[index], recv_sem=recv_sem.at[index],
            device_id=device, device_id_type=MESH,
        )

    barrier = pltpu.get_barrier_semaphore()
    for device in (partner, x_up, x_down, z_up, z_down, cross_up, cross_down):
        pl.semaphore_signal(barrier, inc=1, device_id=device, device_id_type=MESH)

    lane = lax.broadcasted_iota(jnp.int32, (F, L), 1)
    zlane = lane & 15
    first, last = zlane == 0, zlane == 15
    half96 = lax.broadcasted_iota(jnp.int32, (B, L), 1) < 64
    zlane8 = lax.broadcasted_iota(jnp.int32, (8, L), 1) & 15

    perm[...] = one_hot((512, 512), lambda r, c: r == source_of(c))
    spread = one_hot((32, L), lambda r, c: r == (c >> 2))
    coef = coef_ref[...]
    high = coef.astype(BF16)
    low = (coef - high.astype(F32)).astype(BF16)
    coefs[0] = jnp.dot(high, spread, preferred_element_type=F32)
    coefs[1] = jnp.dot(low, spread, preferred_element_type=F32)
    stage[...] = jnp.zeros_like(stage)

    def enter(x):
        for yp in range(2):
            for y in range(4):
                row = x * 8 + 2 * y + yp
                stage[0:Q, y * L : y * L + L] = b_ref[pl.ds(row, Q, 32), :]
                stage[Q : Q + 1, y * L : y * L + L] = coefs[0, pl.ds(row, 1), :]
                stage[Q + 1 : Q + 2, y * L : y * L + L] = coefs[1, pl.ds(row, 1), :]
            ordered = jnp.dot(stage[...].astype(BF16), perm[...], preferred_element_type=F32)
            for r in range(4):
                arrive[r, x, yp] = ordered[:, r * L : r * L + L].astype(BF16)

    enter(3)
    pl.semaphore_wait(barrier, 7)
    shifts = [
        copy(SHIFT, arrive.at[pl.ds(2 * gy, 2), 3], xr.at[0], x_up),
        copy(SHIFT + 1, arrive.at[pl.ds(2 * (1 - gy), 2), 3], xr.at[1], cross_up),
    ]
    for c in shifts:
        c.start()

    def enter_rest(x, carry):
        enter(x)
        return carry

    lax.fori_loop(0, 3, enter_rest, 0)
    swap = copy(SWAP, arrive.at[pl.ds(2 * (1 - gy), 2)], partner_in, partner)
    swap.start()

    for i in range(6):
        chunk = p_ref[:, i * L : min(i * L + L, 8 * Q)].astype(F32)
        short = L - chunk.shape[1]
        if short:
            chunk = jnp.concatenate([chunk, jnp.zeros((8 * Q, short), F32)], axis=1)
        p_rows[i] = chunk
    for o in range(8):
        for i in range(6):
            rows = p_rows[i, pl.ds(o, Q, 8), :]
            rows = jnp.concatenate([rows, jnp.zeros((F - Q, L), F32)], axis=0)
            p_stack[o * F : o * F + F, i * L : i * L + L] = rows.astype(BF16)
    for i in range(6):
        p_cols[128 * i : 128 * i + 128, :] = one_hot(
            (128, 8 * B), lambda r, c: r + 128 * i == 8 * (c - 96 * ((c * 683) >> 16)) + ((c * 683) >> 16)
        )
    PINV[...] = jnp.dot(p_stack[...], p_cols[...], preferred_element_type=F32).astype(BF16)
    square[...] = jnp.zeros_like(square)
    weights = jnp.zeros((F, 7 * B), F32)
    for i in range(4):
        square[0:Q, 0:Q] = f_ref[i - 1] if i else m_ref[...]
        whole = square[...]
        parts = [(0, whole)] if i == 0 else [(2 * i - 1, -whole.T), (2 * i, -whole)]
        for at, part in parts:
            place = one_hot((L, 7 * B), lambda r, c: (r + B * at == c) & (r < B))
            weights += jnp.dot(part[:F].astype(BF16), place, preferred_element_type=F32)
    W[...] = weights.astype(BF16)
    S[...] = jnp.zeros_like(S)

    def joined(own, other):
        own, other = own.astype(F32), other.astype(F32)
        lo, hi = jnp.where(gy == 0, own, other), jnp.where(gy == 0, other, own)
        return jnp.where(half96, lo, roll(hi, 64)), jnp.where(half96, roll(lo, 64), hi)

    def keep_coef(xi, yp, zp, tile):
        value = jnp.broadcast_to(tile[Q : Q + 1] + tile[Q + 1 : Q + 2], (8, L))
        CF[xi, yp, zp] = value
        SN[xi, yp, zp] = lax.rsqrt(value)

    swap.wait()

    def place(x, carry):
        for h in range(2):
            for yp in range(2):
                for zp, tile in enumerate(joined(arrive[2 * gy + h, x, yp], partner_in[h, x, yp])):
                    R[h, x, yp, zp] = tile[:F]
                    if h == 0:
                        keep_coef(x + 1, yp, zp, tile)
        return carry

    lax.fori_loop(0, 4, place, 0)
    for c in shifts:
        c.wait()
    for h in range(2):
        for yp in range(2):
            for zp, tile in enumerate(joined(xr[0, h, yp], xr[1, h, yp])):
                R[h, 3, yp, zp] = tile[:F]
                if h == 0:
                    keep_coef(0, yp, zp, tile)

    up, down = jnp.zeros((8, L), F32), jnp.zeros((8, L), F32)
    for xi in range(5):
        for yp in range(2):
            j = 2 * xi + yp
            up = jnp.where(zlane8 == j, roll(SN[xi, yp, 1], j - 15), up)
            down = jnp.where(zlane8 == j, roll(SN[xi, yp, 0], j), down)
    su[...] = up
    sd[...] = down
    s_copies = [copy(SINIT, su, hsl, z_up), copy(SINIT + 1, sd, hsu, z_down)]
    for c in s_copies:
        c.start()

    def slot(l, a):
        return (l + 3 * (1 - a)) % 4 if isinstance(a, int) else lax.rem(l + 3 * (1 - a), 4)

    def times(ref, index, tile):
        return ref[index][0:1] * tile

    def pre_copies(h):
        return (
            copy(PRE + 2 * h, PU.at[h], HL.at[h], z_up),
            copy(PRE + 2 * h + 1, PD.at[h], HU.at[h], z_down),
        )

    def x_copy(h, g, a, way):
        if way:
            return copy(POSTX + 4 * h + 2 * g + 1, CB.at[h, slot(0, a)], XU.at[h, g], x_down)
        return copy(POSTX + 4 * h + 2 * g, CB.at[h, slot(3, a)], XL.at[h, g], x_up)

    def z_copies(h):
        return (
            copy(POSTZ + 2 * h, QU.at[h], GL.at[h], z_up),
            copy(POSTZ + 2 * h + 1, QD.at[h], GU.at[h], z_down),
        )

    def mid_copy(h, which):
        return copy(MID + 2 * h + which, MS.at[h, which], MR.at[h, which], x_down)

    def out_copy(w, h):
        return copy(OUTS + 2 * w + h, OS.at[w, h], OIN.at[w, 2 * gy + h], partner)

    def pre(h, a):
        up, down = jnp.zeros((F, L), F32), jnp.zeros((F, L), F32)
        for l in range(4):
            for yp in range(2):
                j = 2 * l + yp
                tile = times(SN, (l + a, yp, 1), R[h, slot(l, a), yp, 1])
                up = jnp.where(zlane == j, roll(tile, j - 15), up)
                tile = times(SN, (l + a, yp, 0), R[h, slot(l, a), yp, 0])
                down = jnp.where(zlane == j, roll(tile, j), down)
        PU[h] = padded(up)
        PD[h] = padded(down)
        for c in pre_copies(h):
            c.start()

    def frames(b, g):
        for dx in range(2):
            for dy in range(2):
                for dz in range(2):
                    yp, zp = (dy if b else 1 - dy), (dz if g else 1 - dz)
                    ry, rz = int(not b and dy == 0), int(not g and dz == 0)
                    yield 4 * dx + 2 * dy + dz, dx, yp, zp, ry, rz

    def solve(h, a, b, g):
        if g == 0:
            for c in pre_copies(h):
                c.wait_recv()
        for k, dx, yp, zp, ry, rz in frames(b, g):
            for X in range(2):
                l = 2 * X + dx
                tile = times(SN, (l + a, yp, zp), R[h, slot(l, a), yp, zp])
                tile = roll(tile, 16 * ry + rz)
                if rz:
                    ghost = roll(HL[h].astype(F32)[:F], 16 * ry - (2 * l + yp))
                    tile = jnp.where(first, ghost, tile)
                XK[k * B : k * B + B, X * L : X * L + L] = padded(tile)
            if g == 0:
                edge = (PU if rz else HU)[h].astype(F32)
                XK[k * B : k * B + B, 2 * L : 3 * L] = roll(edge, 16 * ry - (2 * dx + yp)).astype(BF16)
        width = 256 if g else 384
        OUT[:, :width] = jnp.dot(PINV[...], XK[:, :width], preferred_element_type=F32)
        if g == 0:
            for c in pre_copies(h):
                c.wait_send()
        up, down = jnp.zeros((F, L), F32), jnp.zeros((F, L), F32)
        for X in range(2):
            for k, dx, yp, zp, ry, rz in frames(b, g):
                l = 2 * X + dx
                j = 2 * l + yp
                s = slot(l, a)
                block = OUT[k * F : k * F + F, X * L : X * L + L]
                if g:
                    corr = times(SN, (l + a, yp, zp), roll(block, -16 * ry))
                    if zp:
                        up = jnp.where(zlane == j, roll(corr, j - 15), up)
                        beside = roll(corr, 1)
                    else:
                        down = jnp.where(zlane == j, roll(corr, j), down)
                        beside = roll(corr, -1)
                else:
                    edge = OUT[k * F : k * F + F, 2 * L : 3 * L]
                    here = roll(block, -16 * ry)
                    above = jnp.where(last, roll(edge, 15 - 4 * X - 16 * ry), roll(block, -16 * ry - 1))
                    if zp:
                        corr = times(SN, (l + a, yp, 1), above)
                        beside = times(SOM, (l + a, yp), here)
                    else:
                        corr = times(SN, (l + a, yp, 0), here)
                        beside = times(SEP, (l + a, yp), above)
                S[h, s, yp, zp] += corr
                CB[h, s, yp, zp] = padded(corr)
                DB[h, s, yp, zp] = padded(times(CF, (l + a, yp, zp), corr))
                YR[h, s, yp, zp] = padded(roll(corr, 16 if yp else -16))
                ZR[h, s, yp, zp] = padded(beside)
            x_copy(h, g, a, 1 - X).start()
        if g:
            QU[h] = padded(up)
            QD[h] = padded(down)
            for c in z_copies(h):
                c.start()

    def update(h, a, g):
        if g:
            for c in z_copies(h):
                c.wait_recv()
        for l in (1, 2, 0, 3):
            if l == 0:
                x_copy(h, g, a, 0).wait_recv()
            if l == 3:
                x_copy(h, g, a, 1).wait_recv()
            s = slot(l, a)
            for yp in range(2):
                j = 2 * l + yp
                pair = lambda ref, *index: [ref[(*index, 0)], ref[(*index, 1)]]
                own = pair(CB, h, s, yp)
                behind, ahead = ZR[h, s, yp, 1], ZR[h, s, yp, 0]
                if g:
                    ghost = roll(GL[h].astype(F32)[:F], -j)
                    behind = padded(jnp.where(first, ghost, behind.astype(F32)[:F]))
                    ghost = roll(GU[h].astype(F32)[:F], 15 - j)
                    ahead = padded(jnp.where(last, ghost, ahead.astype(F32)[:F]))
                blocks = [
                    pair(DB, h, s, yp),
                    pair(CB, h, slot(l - 1, a), yp) if l else pair(XL, h, g, yp),
                    pair(CB, h, slot(l + 1, a), yp) if l < 3 else pair(XU, h, g, yp),
                    pair(CB, h, s, 0) if yp else pair(YR, h, s, 1),
                    pair(YR, h, s, 0) if yp else pair(CB, h, s, 1),
                    [behind, own[0]],
                    [own[1], ahead],
                ]
                stacked = jnp.concatenate([jnp.concatenate(block, axis=1) for block in blocks], axis=0)
                change = jnp.dot(W[...], stacked, preferred_element_type=F32)
                R[h, s, yp, 0] -= change[:, :L]
                R[h, s, yp, 1] -= change[:, L:]
        for c in (x_copy(h, g, a, 0), x_copy(h, g, a, 1)) + (z_copies(h) if g else ()):
            c.wait_send()

    def leave(w, h, field):
        def one(x, carry):
            for yp in range(2):
                even, odd = field[h, x, yp, 0], field[h, x, yp, 1]
                lo = jnp.where(lane < 64, even, roll(odd, 64))
                hi = jnp.where(lane < 64, roll(even, 64), odd)
                OIN[w, 2 * gy + h, x, yp] = padded(jnp.where(gy == 0, lo, hi))
                OS[w, h, x, yp] = padded(jnp.where(gy == 0, hi, lo))
            return carry

        lax.fori_loop(0, 4, one, 0)
        out_copy(w, h).start()

    for h in range(2):
        pre(h, 0)
    for c in s_copies:
        c.wait()
    for xi in range(5):
        for yp in range(2):
            j = 2 * xi + yp
            SEP[xi, yp] = jnp.where(zlane8 == 15, roll(hsu[...], 15 - j), roll(SN[xi, yp, 0], -1))
            SOM[xi, yp] = jnp.where(zlane8 == 0, roll(hsl[...], -j), roll(SN[xi, yp, 1], 1))

    def round_of_four(a, carry):
        for b in range(2):
            for h in range(2):
                solve(h, a, b, 0)
            for h in range(2):
                update(h, a, 0)
                solve(h, a, b, 1)
            if b == 0:
                for h in range(2):
                    update(h, a, 1)
                    pre(h, a)

        @pl.when(a == 1)
        def _():
            for h in range(2):
                mid_copy(h, 1).wait()
                for yp in range(2):
                    for zp in range(2):
                        S[h, 3, yp, zp] += MR[h, 1, yp, zp][:F].astype(F32)
                leave(0, h, S)

        for h in range(2):
            update(h, a, 1)

            @pl.when(a == 0)
            def _():
                for which, field in enumerate((R, S)):
                    for yp in range(2):
                        for zp in range(2):
                            MS[h, which, yp, zp] = padded(field[h, 3, yp, zp])
                    mid_copy(h, which).start()
                S[h, 3] = jnp.zeros((2, 2, F, L), F32)

        @pl.when(a == 0)
        def _():
            for h in range(2):
                mid_copy(h, 0).wait()
                for yp in range(2):
                    for zp in range(2):
                        R[h, 3, yp, zp] = MR[h, 0, yp, zp][:F].astype(F32)
                pre(h, 1)

        return carry

    lax.fori_loop(0, 2, round_of_four, 0)
    for h in range(2):
        leave(1, h, R)
    stores = [pltpu.make_async_copy(OIN.at[w], out_ref.at[w], out_sem.at[w]) for w in range(2)]
    for w in range(2):
        for h in range(2):
            out_copy(w, h).wait()
        stores[w].start()
    for c in stores:
        c.wait()


def finish(in_ref, sol_ref, res_ref, perm):
    perm[...] = one_hot((512, 512), lambda r, c: source_of(r) == c)
    for w, out_ref in enumerate((sol_ref, res_ref)):

        def one(x, carry):
            for yp in range(2):
                tiles = jnp.concatenate([in_ref[w, r, x, yp] for r in range(4)], axis=1)
                back = jnp.dot(tiles, perm[...], preferred_element_type=F32)
                for y in range(4):
                    out_ref[pl.ds(x * 8 + 2 * y + yp, Q, 32), :] = back[:Q, y * L : y * L + L]
            return carry

        lax.fori_loop(0, 4, one, 0)


def on_device(nx, nz, right_side, cell_coef, cell_matrix, face_coupling, patch_inverse):
    flat = right_side.reshape(-1, L)
    tile = lambda *dims, t=BF16: pltpu.VMEM((*dims, B if t == BF16 else F, L), t)
    vmem = pl.BlockSpec(memory_space=pltpu.VMEM)
    ordered = pl.pallas_call(
        functools.partial(kernel, nx, nz),
        out_shape=jax.ShapeDtypeStruct((2, 4, 4, 2, B, L), BF16),
        in_specs=[vmem] * 5,
        out_specs=pl.BlockSpec(memory_space=pl.ANY),
        scratch_shapes=[
            pltpu.VMEM((512, 512), BF16),
            pltpu.VMEM((B, 512), F32),
            pltpu.VMEM((2, 32, L), F32),
            pltpu.VMEM((6, 8 * Q, L), F32),
            pltpu.VMEM((8 * B, 8 * B), BF16),
            pltpu.VMEM((8 * F, 8 * B), BF16),
            pltpu.VMEM((8 * F, 8 * B), BF16),
            pltpu.VMEM((L, L), F32),
            pltpu.VMEM((F, 7 * B), BF16),
            tile(4, 4, 2),
            tile(2, 4, 2),
            tile(2, 4, 2, 2, t=F32),
            tile(2, 4, 2, 2, t=F32),
            pltpu.VMEM((5, 2, 2, 8, L), F32),
            pltpu.VMEM((5, 2, 2, 8, L), F32),
            pltpu.VMEM((5, 2, 8, L), F32),
            pltpu.VMEM((5, 2, 8, L), F32),
            *[pltpu.VMEM((8, L), F32)] * 4,
            tile(2, 2, 2),
            pltpu.VMEM((8 * B, 3 * L), BF16),
            pltpu.VMEM((8 * F, 3 * L), F32),
            *[tile(2, 4, 2, 2)] * 4,
            *[tile(2, 2, 2, 2)] * 2,
            *[tile(2)] * 8,
            *[tile(2, 2, 2, 2)] * 2,
            tile(2, 4, 4, 2),
            tile(2, 2, 4, 2),
            pltpu.SemaphoreType.DMA((COPIES,)),
            pltpu.SemaphoreType.DMA((COPIES,)),
            pltpu.SemaphoreType.DMA((2,)),
        ],
        compiler_params=pltpu.CompilerParams(
            collective_id=0, has_side_effects=True, vmem_limit_bytes=48 * 1024 * 1024
        ),
    )(flat, cell_coef.reshape(32, 32), patch_inverse, cell_matrix, face_coupling)
    sol, res = pl.pallas_call(
        finish,
        out_shape=[jax.ShapeDtypeStruct(flat.shape, F32)] * 2,
        in_specs=[vmem],
        out_specs=[vmem] * 2,
        scratch_shapes=[pltpu.VMEM((512, 512), BF16)],
    )(ordered)
    return sol.reshape(right_side.shape), res.reshape(right_side.shape)


def solution(mesh):
    fields = P(None, "gx", "gy", "gz")
    return jax.shard_map(
        functools.partial(on_device, mesh.shape["gx"], mesh.shape["gz"]),
        mesh=mesh,
        in_specs=(fields, P("gx", "gy", "gz"), P(), P(), P()),
        out_specs=(fields, fields),
        check_vma=False,
    )
```

time: 156 us -> 114 us (0.73)
  local copies, waits for them, and re-layouts: 34.1 us -> 6.08 us
  Pallas kernels: 121 us -> 107 us
    reshape x2 -> x0, local copies, waits for them, and re-layouts: 15.9 us -> none  [the longest x1 13.8 us: on_device(): blocks = patch_inverse.reshape(Q, 8, Q, 8).transpose(1, 0, 3, 2)]
    pallas_call x1 -> x2, Pallas kernels: 121 us -> 107 us  [the longest x1 101 us: on_device(): pl.pallas_call(functools.partial(kernel, nx, nz), out_shape=jax.ShapeDtyp...]
    unnamed x13 -> x12, local copies, waits for them, and re-layouts: 16.1 us -> 6.08 us
where the time goes in v2:
time: 114 us; the launch traced here: 113 us
  Pallas kernels  107 us (94%)
  local copies, waits for them, and re-layouts  6.08 us (5%)
    pallas_call x1, Pallas kernels, on_device(): pl.pallas_call(functools.partial(kernel, nx, nz), out_shape=jax.ShapeDtyp...  101 us
    unnamed x12, local copies, waits for them, and re-layouts  6.08 us
    pallas_call x1, Pallas kernels, on_device(): pl.pallas_call(finish, out_shape=[jax.ShapeDtypeStruct(flat.shape, F32)]...  5.84 us

profile of v2, /device:TPU:1, one launch (start us, length us, event | category | flops | bytes accessed | tf_op | source)
XLA Modules:
  0.0 113.5 jit_solution(8532569342487051188)
XLA Ops:
  0.6 0.0 copy-start.1
  0.6 1.3 %copy-done.1 = f32[81,4,8,128]{3,2,1,0:T(8,128)S(1)} copy-done((f32[81,4,8,128]{3,2,1,0:T(8,128)S(1)}, f32[81,4,8,128]{3,2,1,0:T(8,128)}, u32[]{:S(2)}) %copy-start.1) | copy-done | bytes 1327128
  2.0 0.0 copy-start.2
  2.0 1.2 %copy-done.2 = bf16[648,648]{1,0:T(8,128)(2,1)S(1)} copy-done((bf16[648,648]{1,0:T(8,128)(2,1)S(1)}, bf16[648,648]{1,0:T(8,128)(2,1)}, u32[]{:S(2)}) %copy-start.2) | copy-done | bytes 839832
  3.2 0.0 copy-start.3
  3.2 0.9 copy-done.3
  4.1 0.0 copy-start.4
  4.1 0.8 copy-done.4
  4.9 0.0 copy-start.5
  4.9 0.7 copy-done.5
  5.6 100.9 %shard_map.68.in_ref = bf16[2,4,4,2,96,128]{5,4,3,2,1,0:T(8,128)(2,1)S(1)} custom-call(f32[2592,128]{1,0:T(8,128)S(1)} %bitcast.4, f32[32,32]{1,0:T(8,128)S(1)} %bitcast.5, bf16[648,648]{1,0:T(8,128)(2,1)S(1)} %copy-done.2, f32[81,81]{1,0:T(8,128)S(1)} %copy-done.4, f32[3,81,81]{2,1,0:T(8,128)S(1)} %copy-done.3), custom_call_target="tpu_custom_call" | custom-call | tf_op jit(solution)/shard_map/pallas_call | solution.py:422
  106.5 0.0 copy-start
  106.5 1.1 %copy-done = bf16[2,4,4,2,96,128]{5,4,3,2,1,0:T(8,128)(2,1)} copy-done((bf16[2,4,4,2,96,128]{5,4,3,2,1,0:T(8,128)(2,1)}, bf16[2,4,4,2,96,128]{5,4,3,2,1,0:T(8,128)(2,1)S(1)}, u32[]{:S(2)}) %copy-start) | copy-done | bytes 1572888
  107.6 5.8 %shard_map.69 = (f32[2592,128]{1,0:T(8,128)}, f32[2592,128]{1,0:T(8,128)}) custom-call(bf16[2,4,4,2,96,128]{5,4,3,2,1,0:T(8,128)(2,1)} %copy-done), custom_call_target="tpu_custom_call" | custom-call | tf_op jit(solution)/shard_map/pallas_call | solution.py:463
Async XLA Ops:
  0.6 1.3 %copy-start.1 = (f32[81,4,8,128]{3,2,1,0:T(8,128)S(1)}, f32[81,4,8,128]{3,2,1,0:T(8,128)}, u32[]{:S(2)}) copy-start(f32[81,4,8,128]{3,2,1,0:T(8,128)} %param.5) | copy-start | bytes 3981316
  2.0 1.2 %copy-start.2 = (bf16[648,648]{1,0:T(8,128)(2,1)S(1)}, bf16[648,648]{1,0:T(8,128)(2,1)}, u32[]{:S(2)}) copy-start(bf16[648,648]{1,0:T(8,128)(2,1)} %p_ref.1) | copy-start | bytes 2519428
  3.2 0.9 copy-start.3
  4.1 0.8 copy-start.4
  4.9 0.7 copy-start.5
  106.5 1.2 %copy-start = (bf16[2,4,4,2,96,128]{5,4,3,2,1,0:T(8,128)(2,1)}, bf16[2,4,4,2,96,128]{5,4,3,2,1,0:T(8,128)(2,1)S(1)}, u32[]{:S(2)}) copy-start(bf16[2,4,4,2,96,128]{5,4,3,2,1,0:T(8,128)(2,1)S(1)} %shard_map.68.in_ref) | copy-start | bytes 4718596

commit v3 on v2

--- a/solution.py
+++ b/solution.py
@@ -14,7 +14,7 @@
 F32, BF16 = jnp.float32, jnp.bfloat16
 MESH = pl.DeviceIdType.MESH
 
-SWAP, SINIT, SHIFT, PRE, POSTX, POSTZ, MID, OUTS, COPIES = 0, 1, 3, 5, 9, 17, 21, 25, 29
+SWAP, SINIT, SHIFT, PRE, POSTX, POSTZ, MID, OUTS, SLANT, COPIES = 0, 1, 3, 5, 9, 17, 21, 25, 29, 33
 
 
 def padded(tile):
@@ -38,12 +38,12 @@
 
 def kernel(
     nx, nz,
-    b_ref, coef_ref, p_ref, m_ref, f_ref,
+    b_any, coef_any, p_any, m_any, f_any,
     out_ref,
-    perm, stage, coefs, p_rows, p_cols, p_stack, PINV, square, W,
+    b_ref, coef_ref, p_ref, m_ref, f_ref, perm, stage, coefs, p_rows, p_cols, p_stack, PINV, square, W, W_LOW, W_HIGH, W_BELOW, W_ABOVE,
     arrive, partner_in, R, S, SN, CF, SEP, SOM, su, sd, hsl, hsu,
-    xr, XK, OUT, CB, DB, YR, ZR, XL, XU, PU, PD, HL, HU, QU, QD, GL, GU, MS, MR, OIN, OS,
-    send_sem, recv_sem, out_sem,
+    xr, XK, OUT, CB, DB, YR, ZR, XL, XU, PU, PD, HL, HU, QU, QD, GL, GU, HLX, HUX, MS, MR, OIN, OS,
+    send_sem, recv_sem, load_sem, out_sem,
 ):
     gx, gy, gz = lax.axis_index("gx"), lax.axis_index("gy"), lax.axis_index("gz")
     up_x, down_x = lax.rem(gx + 1, nx), lax.rem(gx + nx - 1, nx)
@@ -58,8 +58,20 @@
             device_id=device, device_id_type=MESH,
         )
 
+    loads = [
+        pltpu.make_async_copy(src, dst, load_sem.at[i])
+        for i, (src, dst) in enumerate(
+            ((coef_any, coef_ref), (b_any, b_ref), (p_any, p_ref), (m_any, m_ref), (f_any, f_ref))
+        )
+    ]
+    for c in loads:
+        c.start()
+    slant_up, slant_down = (down_x, gy, z_up[2]), (down_x, gy, z_down[2])
     barrier = pltpu.get_barrier_semaphore()
-    for device in (partner, x_up, x_down, z_up, z_down, cross_up, cross_down):
+    for device in (
+        partner, x_up, x_down, z_up, z_down, cross_up, cross_down,
+        slant_up, slant_down, (up_x, gy, z_up[2]), (up_x, gy, z_down[2]),
+    ):
         pl.semaphore_signal(barrier, inc=1, device_id=device, device_id_type=MESH)
 
     lane = lax.broadcasted_iota(jnp.int32, (F, L), 1)
@@ -70,6 +82,7 @@
 
     perm[...] = one_hot((512, 512), lambda r, c: r == source_of(c))
     spread = one_hot((32, L), lambda r, c: r == (c >> 2))
+    loads[0].wait()
     coef = coef_ref[...]
     high = coef.astype(BF16)
     low = (coef - high.astype(F32)).astype(BF16)
@@ -88,8 +101,9 @@
             for r in range(4):
                 arrive[r, x, yp] = ordered[:, r * L : r * L + L].astype(BF16)
 
+    loads[1].wait()
     enter(3)
-    pl.semaphore_wait(barrier, 7)
+    pl.semaphore_wait(barrier, 11)
     shifts = [
         copy(SHIFT, arrive.at[pl.ds(2 * gy, 2), 3], xr.at[0], x_up),
         copy(SHIFT + 1, arrive.at[pl.ds(2 * (1 - gy), 2), 3], xr.at[1], cross_up),
@@ -105,6 +119,8 @@
     swap = copy(SWAP, arrive.at[pl.ds(2 * (1 - gy), 2)], partner_in, partner)
     swap.start()
 
+    for c in loads[2:]:
+        c.wait()
     for i in range(6):
         chunk = p_ref[:, i * L : min(i * L + L, 8 * Q)].astype(F32)
         short = L - chunk.shape[1]
@@ -126,11 +142,16 @@
     for i in range(4):
         square[0:Q, 0:Q] = f_ref[i - 1] if i else m_ref[...]
         whole = square[...]
-        parts = [(0, whole)] if i == 0 else [(2 * i - 1, -whole.T), (2 * i, -whole)]
+        below, above = (0, 6) if i == 1 else (2 * i - 2, 2 * i - 1)
+        parts = [(1, whole)] if i == 0 else [(below, -whole.T), (above, -whole)]
         for at, part in parts:
             place = one_hot((L, 7 * B), lambda r, c: (r + B * at == c) & (r < B))
             weights += jnp.dot(part[:F].astype(BF16), place, preferred_element_type=F32)
     W[...] = weights.astype(BF16)
+    W_LOW[...] = weights[:, B:].astype(BF16)
+    W_HIGH[...] = weights[:, : 6 * B].astype(BF16)
+    W_BELOW[...] = weights[:, :B].astype(BF16)
+    W_ABOVE[...] = weights[:, 6 * B :].astype(BF16)
     S[...] = jnp.zeros_like(S)
 
     def joined(own, other):
@@ -204,6 +225,12 @@
 
     def out_copy(w, h):
         return copy(OUTS + 2 * w + h, OS.at[w, h], OIN.at[w, 2 * gy + h], partner)
+
+    def slant_copies(h):
+        return (
+            copy(SLANT + 2 * h, PU.at[h], HLX.at[h], slant_up),
+            copy(SLANT + 2 * h + 1, PD.at[h], HUX.at[h], slant_down),
+        )
 
     def pre(h, a):
         up, down = jnp.zeros((F, L), F32), jnp.zeros((F, L), F32)
@@ -228,9 +255,6 @@
                     yield 4 * dx + 2 * dy + dz, dx, yp, zp, ry, rz
 
     def solve(h, a, b, g):
-        if g == 0:
-            for c in pre_copies(h):
-                c.wait_recv()
         for k, dx, yp, zp, ry, rz in frames(b, g):
             for X in range(2):
                 l = 2 * X + dx
@@ -245,12 +269,11 @@
                 XK[k * B : k * B + B, 2 * L : 3 * L] = roll(edge, 16 * ry - (2 * dx + yp)).astype(BF16)
         width = 256 if g else 384
         OUT[:, :width] = jnp.dot(PINV[...], XK[:, :width], preferred_element_type=F32)
-        if g == 0:
-            for c in pre_copies(h):
-                c.wait_send()
         up, down = jnp.zeros((F, L), F32), jnp.zeros((F, L), F32)
-        for X in range(2):
+        for X, side in ((0, 0), (1, 1), (0, 1), (1, 0)):
             for k, dx, yp, zp, ry, rz in frames(b, g):
+                if dx != side:
+                    continue
                 l = 2 * X + dx
                 j = 2 * l + yp
                 s = slot(l, a)
@@ -278,27 +301,32 @@
                 DB[h, s, yp, zp] = padded(times(CF, (l + a, yp, zp), corr))
                 YR[h, s, yp, zp] = padded(roll(corr, 16 if yp else -16))
                 ZR[h, s, yp, zp] = padded(beside)
-            x_copy(h, g, a, 1 - X).start()
+            if X == side:
+                x_copy(h, g, a, 1 - X).start()
         if g:
             QU[h] = padded(up)
             QD[h] = padded(down)
             for c in z_copies(h):
                 c.start()
 
+    def pair(ref, *index):
+        return jnp.concatenate([ref[(*index, 0)], ref[(*index, 1)]], axis=1)
+
+    def subtract(h, s, yp, weights, blocks):
+        stacked = jnp.concatenate(blocks, axis=0) if len(blocks) > 1 else blocks[0]
+        change = jnp.dot(weights[...], stacked, preferred_element_type=F32)
+        R[h, s, yp, 0] -= change[:, :L]
+        R[h, s, yp, 1] -= change[:, L:]
+
     def update(h, a, g):
         if g:
             for c in z_copies(h):
                 c.wait_recv()
-        for l in (1, 2, 0, 3):
-            if l == 0:
-                x_copy(h, g, a, 0).wait_recv()
-            if l == 3:
-                x_copy(h, g, a, 1).wait_recv()
+        for l in (0, 3, 1, 2):
             s = slot(l, a)
             for yp in range(2):
                 j = 2 * l + yp
-                pair = lambda ref, *index: [ref[(*index, 0)], ref[(*index, 1)]]
-                own = pair(CB, h, s, yp)
+                even, odd = CB[h, s, yp, 0], CB[h, s, yp, 1]
                 behind, ahead = ZR[h, s, yp, 1], ZR[h, s, yp, 0]
                 if g:
                     ghost = roll(GL[h].astype(F32)[:F], -j)
@@ -307,17 +335,20 @@
                     ahead = padded(jnp.where(last, ghost, ahead.astype(F32)[:F]))
                 blocks = [
                     pair(DB, h, s, yp),
-                    pair(CB, h, slot(l - 1, a), yp) if l else pair(XL, h, g, yp),
-                    pair(CB, h, slot(l + 1, a), yp) if l < 3 else pair(XU, h, g, yp),
                     pair(CB, h, s, 0) if yp else pair(YR, h, s, 1),
                     pair(YR, h, s, 0) if yp else pair(CB, h, s, 1),
-                    [behind, own[0]],
-                    [own[1], ahead],
+                    jnp.concatenate([behind, even], axis=1),
+                    jnp.concatenate([odd, ahead], axis=1),
                 ]
-                stacked = jnp.concatenate([jnp.concatenate(block, axis=1) for block in blocks], axis=0)
-                change = jnp.dot(W[...], stacked, preferred_element_type=F32)
-                R[h, s, yp, 0] -= change[:, :L]
-                R[h, s, yp, 1] -= change[:, L:]
+                if l:
+                    blocks = [pair(CB, h, slot(l - 1, a), yp)] + blocks
+                if l < 3:
+                    blocks = blocks + [pair(CB, h, slot(l + 1, a), yp)]
+                subtract(h, s, yp, {0: W_LOW, 3: W_HIGH}.get(l, W), blocks)
+        for way, (l, ghost, weights) in enumerate(((3, XL, W_BELOW), (0, XU, W_ABOVE))):
+            x_copy(h, g, a, way).wait_recv()
+            for yp in range(2):
+                subtract(h, slot(3 - l, a), yp, weights, [pair(ghost, h, g, yp)])
         for c in (x_copy(h, g, a, 0), x_copy(h, g, a, 1)) + (z_copies(h) if g else ()):
             c.wait_send()
 
@@ -347,6 +378,16 @@
     def round_of_four(a, carry):
         for b in range(2):
             for h in range(2):
+                if b:
+                    for c in pre_copies(h):
+                        c.wait()
+                else:
+
+                    @pl.when(a == 0)
+                    def _():
+                        for c in pre_copies(h):
+                            c.wait()
+
                 solve(h, a, b, 0)
             for h in range(2):
                 update(h, a, 0)
@@ -375,16 +416,28 @@
                         for zp in range(2):
                             MS[h, which, yp, zp] = padded(field[h, 3, yp, zp])
                     mid_copy(h, which).start()
+                    if which == 0:
+                        pre(h, 0)
+                        for c in slant_copies(h):
+                            c.start()
                 S[h, 3] = jnp.zeros((2, 2, F, L), F32)
 
         @pl.when(a == 0)
         def _():
             for h in range(2):
                 mid_copy(h, 0).wait()
+                top = jnp.zeros((F, L), F32)
                 for yp in range(2):
                     for zp in range(2):
                         R[h, 3, yp, zp] = MR[h, 0, yp, zp][:F].astype(F32)
-                pre(h, 1)
+                    tile = times(SN, (4, yp, 1), MR[h, 0, yp, 1][:F].astype(F32))
+                    top = jnp.where(zlane == 6 + yp, roll(tile, yp - 9), top)
+                for c in pre_copies(h) + slant_copies(h):
+                    c.wait()
+                for edge, upper in ((HL, HLX[h].astype(F32)[:F]), (HU, HUX[h].astype(F32)[:F]), (PU, None)):
+                    lower = roll(edge[h].astype(F32)[:F], -2)
+                    upper = top if upper is None else roll(upper, 6)
+                    edge[h] = padded(jnp.where(zlane < 6, lower, jnp.where(zlane < 8, upper, 0.0)))
 
         return carry
 
@@ -400,31 +453,47 @@
         c.wait()
 
 
-def finish(in_ref, sol_ref, res_ref, perm):
+def finish(in_any, sol_any, res_any, in_ref, sol_ref, res_ref, perm, in_sem, out_sem):
+    loads = [pltpu.make_async_copy(in_any.at[w], in_ref.at[w], in_sem.at[w]) for w in range(2)]
+    for c in loads:
+        c.start()
     perm[...] = one_hot((512, 512), lambda r, c: source_of(r) == c)
-    for w, out_ref in enumerate((sol_ref, res_ref)):
+    outs = ((sol_ref, sol_any), (res_ref, res_any))
+    stores = [pltpu.make_async_copy(src, dst, out_sem.at[w]) for w, (src, dst) in enumerate(outs)]
+    for w, (out_ref, _) in enumerate(outs):
+        loads[w].wait()
 
         def one(x, carry):
+            tiles = jnp.concatenate(
+                [jnp.concatenate([in_ref[w, r, x, yp] for r in range(4)], axis=1) for yp in range(2)], axis=0
+            )
+            back = jnp.dot(tiles, perm[...], preferred_element_type=F32)
             for yp in range(2):
-                tiles = jnp.concatenate([in_ref[w, r, x, yp] for r in range(4)], axis=1)
-                back = jnp.dot(tiles, perm[...], preferred_element_type=F32)
                 for y in range(4):
-                    out_ref[pl.ds(x * 8 + 2 * y + yp, Q, 32), :] = back[:Q, y * L : y * L + L]
+                    out_ref[pl.ds(x * 8 + 2 * y + yp, Q, 32), :] = back[yp * B : yp * B + Q, y * L : y * L + L]
             return carry
 
         lax.fori_loop(0, 4, one, 0)
+        stores[w].start()
+    for c in stores:
+        c.wait()
 
 
 def on_device(nx, nz, right_side, cell_coef, cell_matrix, face_coupling, patch_inverse):
     flat = right_side.reshape(-1, L)
     tile = lambda *dims, t=BF16: pltpu.VMEM((*dims, B if t == BF16 else F, L), t)
-    vmem = pl.BlockSpec(memory_space=pltpu.VMEM)
+    whole = pl.BlockSpec(memory_space=pl.ANY)
     ordered = pl.pallas_call(
         functools.partial(kernel, nx, nz),
         out_shape=jax.ShapeDtypeStruct((2, 4, 4, 2, B, L), BF16),
-        in_specs=[vmem] * 5,
-        out_specs=pl.BlockSpec(memory_space=pl.ANY),
+        in_specs=[whole] * 5,
+        out_specs=whole,
         scratch_shapes=[
+            pltpu.VMEM(flat.shape, F32),
+            pltpu.VMEM((32, 32), F32),
+            pltpu.VMEM((8 * Q, 8 * Q), BF16),
+            pltpu.VMEM((Q, Q), F32),
+            pltpu.VMEM((3, Q, Q), F32),
             pltpu.VMEM((512, 512), BF16),
             pltpu.VMEM((B, 512), F32),
             pltpu.VMEM((2, 32, L), F32),
@@ -434,6 +503,8 @@
             pltpu.VMEM((8 * F, 8 * B), BF16),
             pltpu.VMEM((L, L), F32),
             pltpu.VMEM((F, 7 * B), BF16),
+            *[pltpu.VMEM((F, 6 * B), BF16)] * 2,
+            *[pltpu.VMEM((F, B), BF16)] * 2,
             tile(4, 4, 2),
             tile(2, 4, 2),
             tile(2, 4, 2, 2, t=F32),
@@ -448,24 +519,32 @@
             pltpu.VMEM((8 * F, 3 * L), F32),
             *[tile(2, 4, 2, 2)] * 4,
             *[tile(2, 2, 2, 2)] * 2,
-            *[tile(2)] * 8,
+            *[tile(2)] * 10,
             *[tile(2, 2, 2, 2)] * 2,
             tile(2, 4, 4, 2),
             tile(2, 2, 4, 2),
             pltpu.SemaphoreType.DMA((COPIES,)),
             pltpu.SemaphoreType.DMA((COPIES,)),
+            pltpu.SemaphoreType.DMA((5,)),
             pltpu.SemaphoreType.DMA((2,)),
         ],
         compiler_params=pltpu.CompilerParams(
-            collective_id=0, has_side_effects=True, vmem_limit_bytes=48 * 1024 * 1024
+            collective_id=0, has_side_effects=True, vmem_limit_bytes=67043328
         ),
     )(flat, cell_coef.reshape(32, 32), patch_inverse, cell_matrix, face_coupling)
     sol, res = pl.pallas_call(
         finish,
         out_shape=[jax.ShapeDtypeStruct(flat.shape, F32)] * 2,
-        in_specs=[vmem],
-        out_specs=[vmem] * 2,
-        scratch_shapes=[pltpu.VMEM((512, 512), BF16)],
+        in_specs=[whole],
+        out_specs=[whole] * 2,
+        scratch_shapes=[
+            tile(2, 4, 4, 2),
+            *[pltpu.VMEM(flat.shape, F32)] * 2,
+            pltpu.VMEM((512, 512), BF16),
+            pltpu.SemaphoreType.DMA((2,)),
+            pltpu.SemaphoreType.DMA((2,)),
+        ],
+        compiler_params=pltpu.CompilerParams(vmem_limit_bytes=67043328),
     )(ordered)
     return sol.reshape(right_side.shape), res.reshape(right_side.shape)
 

time: 114 us -> 106 us (0.930)
  local copies, waits for them, and re-layouts: 6.08 us -> 0 us
  Pallas kernels: 107 us -> 105 us
    unnamed x12 -> x0, local copies, waits for them, and re-layouts: 6.08 us -> none
    pallas_call x1, Pallas kernels: 101 us -> 99.2 us  [on_device(): pl.pallas_call(functools.partial(kernel, nx, nz), out_shape=jax.ShapeDtyp...]
where the time goes in v3:
time: 106 us
  Pallas kernels  105 us (99%)
    pallas_call x1, Pallas kernels, on_device(): pl.pallas_call(functools.partial(kernel, nx, nz), out_shape=jax.ShapeDtyp...  99.2 us
    pallas_call x1, Pallas kernels, on_device(): pl.pallas_call(finish, out_shape=[jax.ShapeDtypeStruct(flat.shape, F32)]...  5.51 us

profile of v3, /device:TPU:1, one launch (start us, length us, event | category | flops | bytes accessed | tf_op | source)
XLA Modules:
  0.0 105.5 jit_solution(7877235545592162848)
XLA Ops:
  0.6 99.2 %shard_map.68.in_any = bf16[2,4,4,2,96,128]{5,4,3,2,1,0:T(8,128)(2,1)} custom-call(f32[2592,128]{1,0:T(8,128)} %bitcast.4, f32[32,32]{1,0:T(8,128)} %bitcast.5, bf16[648,648]{1,0:T(8,128)(2,1)} %p_any.1, f32[81,81]{1,0:T(8,128)} %m_any.1, f32[3,81,81]{2,1,0:T(8,128)} %f_any.1), custom_call_target="tpu_custom_call" | custom-call | tf_op jit(solution)/shard_map/pallas_call | solution.py:486
  99.8 5.5 %shard_map.69 = (f32[2592,128]{1,0:T(8,128)}, f32[2592,128]{1,0:T(8,128)}) custom-call(bf16[2,4,4,2,96,128]{5,4,3,2,1,0:T(8,128)(2,1)} %shard_map.68.in_any), custom_call_target="tpu_custom_call" | custom-call | tf_op jit(solution)/shard_map/pallas_call | solution.py:535

commit v4 on v3

--- a/solution.py
+++ b/solution.py
@@ -14,7 +14,7 @@
 F32, BF16 = jnp.float32, jnp.bfloat16
 MESH = pl.DeviceIdType.MESH
 
-SWAP, SINIT, SHIFT, PRE, POSTX, POSTZ, MID, OUTS, SLANT, COPIES = 0, 1, 3, 5, 9, 17, 21, 25, 29, 33
+SWAP, SINIT, SHIFT, PRE, POSTX, POSTZ, MID, OUTS, SLANT, RISE, SRISE, COPIES = 0, 1, 3, 5, 9, 17, 21, 25, 29, 33, 37, 39
 
 
 def padded(tile):
@@ -41,7 +41,7 @@
     b_any, coef_any, p_any, m_any, f_any,
     out_ref,
     b_ref, coef_ref, p_ref, m_ref, f_ref, perm, stage, coefs, p_rows, p_cols, p_stack, PINV, square, W, W_LOW, W_HIGH, W_BELOW, W_ABOVE,
-    arrive, partner_in, R, S, SN, CF, SEP, SOM, su, sd, hsl, hsu,
+    arrive, partner_in, R, S, SN, CF, SEP, SOM, su, sd, hsl, hsu, hslx, hsux,
     xr, XK, OUT, CB, DB, YR, ZR, XL, XU, PU, PD, HL, HU, QU, QD, GL, GU, HLX, HUX, MS, MR, OIN, OS,
     send_sem, recv_sem, load_sem, out_sem,
 ):
@@ -176,27 +176,6 @@
         return carry
 
     lax.fori_loop(0, 4, place, 0)
-    for c in shifts:
-        c.wait()
-    for h in range(2):
-        for yp in range(2):
-            for zp, tile in enumerate(joined(xr[0, h, yp], xr[1, h, yp])):
-                R[h, 3, yp, zp] = tile[:F]
-                if h == 0:
-                    keep_coef(0, yp, zp, tile)
-
-    up, down = jnp.zeros((8, L), F32), jnp.zeros((8, L), F32)
-    for xi in range(5):
-        for yp in range(2):
-            j = 2 * xi + yp
-            up = jnp.where(zlane8 == j, roll(SN[xi, yp, 1], j - 15), up)
-            down = jnp.where(zlane8 == j, roll(SN[xi, yp, 0], j), down)
-    su[...] = up
-    sd[...] = down
-    s_copies = [copy(SINIT, su, hsl, z_up), copy(SINIT + 1, sd, hsu, z_down)]
-    for c in s_copies:
-        c.start()
-
     def slot(l, a):
         return (l + 3 * (1 - a)) % 4 if isinstance(a, int) else lax.rem(l + 3 * (1 - a), 4)
 
@@ -365,48 +344,104 @@
         lax.fori_loop(0, 4, one, 0)
         out_copy(w, h).start()
 
+    def each(body):
+        def one(h, carry):
+            body(h)
+            return carry
+
+        lax.fori_loop(0, 2, one, 0)
+
+    rise_up, rise_down = (up_x, gy, z_up[2]), (up_x, gy, z_down[2])
+    up, down = jnp.zeros((8, L), F32), jnp.zeros((8, L), F32)
+    for xi in range(1, 5):
+        for yp in range(2):
+            j = 2 * xi + yp
+            up = jnp.where(zlane8 == j, roll(SN[xi, yp, 1], j - 15), up)
+            down = jnp.where(zlane8 == j, roll(SN[xi, yp, 0], j), down)
+    su[...] = up
+    sd[...] = down
+    s_copies = [
+        copy(SINIT, su, hsl, z_up), copy(SINIT + 1, sd, hsu, z_down),
+        copy(SRISE, su, hslx, rise_up), copy(SRISE + 1, sd, hsux, rise_down),
+    ]
+    for c in s_copies:
+        c.start()
+
+    def rise_copies(h):
+        return (
+            copy(RISE + 2 * h, PU.at[h], HLX.at[h], rise_up),
+            copy(RISE + 2 * h + 1, PD.at[h], HUX.at[h], rise_down),
+        )
+
+    def first_edges(h):
+        pre(h, 1)
+        for c in rise_copies(h):
+            c.start()
+
+    each(first_edges)
+    for c in shifts:
+        c.wait()
     for h in range(2):
-        pre(h, 0)
+        for yp in range(2):
+            for zp, tile in enumerate(joined(xr[0, h, yp], xr[1, h, yp])):
+                R[h, 3, yp, zp] = tile[:F]
+                if h == 0:
+                    keep_coef(0, yp, zp, tile)
     for c in s_copies:
         c.wait()
     for xi in range(5):
         for yp in range(2):
-            j = 2 * xi + yp
-            SEP[xi, yp] = jnp.where(zlane8 == 15, roll(hsu[...], 15 - j), roll(SN[xi, yp, 0], -1))
-            SOM[xi, yp] = jnp.where(zlane8 == 0, roll(hsl[...], -j), roll(SN[xi, yp, 1], 1))
+            lower, upper, j = (hsl, hsu, 2 * xi + yp) if xi else (hslx, hsux, 8 + yp)
+            SEP[xi, yp] = jnp.where(zlane8 == 15, roll(upper[...], 15 - j), roll(SN[xi, yp, 0], -1))
+            SOM[xi, yp] = jnp.where(zlane8 == 0, roll(lower[...], -j), roll(SN[xi, yp, 1], 1))
+
+    def entry_edges(h):
+        for c in pre_copies(h) + rise_copies(h):
+            c.wait()
+        low = jnp.zeros((F, L), F32)
+        for yp in range(2):
+            low = jnp.where(zlane == yp, roll(times(SN, (0, yp, 1), R[h, 3, yp, 1]), yp - 15), low)
+        for edge, beyond in ((HL, HLX), (HU, HUX), (PU, None)):
+            kept = roll(edge[h].astype(F32)[:F], 2)
+            new = low if beyond is None else roll(beyond[h].astype(F32)[:F], -6)
+            edge[h] = padded(jnp.where(zlane < 2, new, jnp.where(zlane < 8, kept, 0.0)))
+
+    each(entry_edges)
 
     def round_of_four(a, carry):
         for b in range(2):
-            for h in range(2):
+
+            def even(h):
                 if b:
                     for c in pre_copies(h):
                         c.wait()
-                else:
-
-                    @pl.when(a == 0)
-                    def _():
-                        for c in pre_copies(h):
-                            c.wait()
-
                 solve(h, a, b, 0)
-            for h in range(2):
+
+            def odd(h):
                 update(h, a, 0)
                 solve(h, a, b, 1)
+
+            def between(h):
+                update(h, a, 1)
+                pre(h, a)
+
+            each(even)
+            each(odd)
             if b == 0:
-                for h in range(2):
-                    update(h, a, 1)
-                    pre(h, a)
+                each(between)
 
         @pl.when(a == 1)
         def _():
-            for h in range(2):
+            def add_shifted(h):
                 mid_copy(h, 1).wait()
                 for yp in range(2):
                     for zp in range(2):
                         S[h, 3, yp, zp] += MR[h, 1, yp, zp][:F].astype(F32)
                 leave(0, h, S)
 
-        for h in range(2):
+            each(add_shifted)
+
+        def end(h):
             update(h, a, 1)
 
             @pl.when(a == 0)
@@ -422,9 +457,15 @@
                             c.start()
                 S[h, 3] = jnp.zeros((2, 2, F, L), F32)
 
+            @pl.when(a == 1)
+            def _():
+                leave(1, h, R)
+
+        each(end)
+
         @pl.when(a == 0)
         def _():
-            for h in range(2):
+            def shifted(h):
                 mid_copy(h, 0).wait()
                 top = jnp.zeros((F, L), F32)
                 for yp in range(2):
@@ -439,11 +480,11 @@
                     upper = top if upper is None else roll(upper, 6)
                     edge[h] = padded(jnp.where(zlane < 6, lower, jnp.where(zlane < 8, upper, 0.0)))
 
+            each(shifted)
+
         return carry
 
     lax.fori_loop(0, 2, round_of_four, 0)
-    for h in range(2):
-        leave(1, h, R)
     stores = [pltpu.make_async_copy(OIN.at[w], out_ref.at[w], out_sem.at[w]) for w in range(2)]
     for w in range(2):
         for h in range(2):
@@ -513,7 +554,7 @@
             pltpu.VMEM((5, 2, 2, 8, L), F32),
             pltpu.VMEM((5, 2, 8, L), F32),
             pltpu.VMEM((5, 2, 8, L), F32),
-            *[pltpu.VMEM((8, L), F32)] * 4,
+            *[pltpu.VMEM((8, L), F32)] * 6,
             tile(2, 2, 2),
             pltpu.VMEM((8 * B, 3 * L), BF16),
             pltpu.VMEM((8 * F, 3 * L), F32),

time: 106 us -> 102 us (0.962)
  Pallas kernels: 105 us -> 101 us
    pallas_call x1, Pallas kernels: 99.2 us -> 95.4 us  [on_device(): pl.pallas_call(functools.partial(kernel, nx, nz), out_shape=jax.ShapeDtyp...]
where the time goes in v4:
time: 102 us
  Pallas kernels  101 us (99%)
    pallas_call x1, Pallas kernels, on_device(): pl.pallas_call(functools.partial(kernel, nx, nz), out_shape=jax.ShapeDtyp...  95.4 us
    pallas_call x1, Pallas kernels, on_device(): pl.pallas_call(finish, out_shape=[jax.ShapeDtypeStruct(flat.shape, F32)]...  5.51 us

profile of v4, /device:TPU:1, one launch (start us, length us, event | category | flops | bytes accessed | tf_op | source)
XLA Modules:
  0.0 101.6 jit_solution(8808041126774491746)
XLA Ops:
  0.6 95.4 %shard_map.68.in_any = bf16[2,4,4,2,96,128]{5,4,3,2,1,0:T(8,128)(2,1)} custom-call(f32[2592,128]{1,0:T(8,128)} %bitcast.4, f32[32,32]{1,0:T(8,128)} %bitcast.5, bf16[648,648]{1,0:T(8,128)(2,1)} %p_any.1, f32[81,81]{1,0:T(8,128)} %m_any.1, f32[3,81,81]{2,1,0:T(8,128)} %f_any.1), custom_call_target="tpu_custom_call" | custom-call | tf_op jit(solution)/shard_map/pallas_call | solution.py:527
  96.0 5.5 %shard_map.69 = (f32[2592,128]{1,0:T(8,128)}, f32[2592,128]{1,0:T(8,128)}) custom-call(bf16[2,4,4,2,96,128]{5,4,3,2,1,0:T(8,128)(2,1)} %shard_map.68.in_any), custom_call_target="tpu_custom_call" | custom-call | tf_op jit(solution)/shard_map/pallas_call | solution.py:576

commit v5 on v4

--- a/solution.py
+++ b/solution.py
@@ -11,6 +11,7 @@
 F = 88
 B = 96
 L = 128
+PITCH = 40
 F32, BF16 = jnp.float32, jnp.bfloat16
 MESH = pl.DeviceIdType.MESH
 
@@ -24,6 +25,10 @@
 def roll(tile, shift):
     shift = shift % L
     return pltpu.roll(tile, shift, 1) if shift else tile
+
+
+def spaced(ref):
+    return ref.reshape(Q, PITCH, L).at[:, :32, :]
 
 
 def one_hot(shape, hit):
@@ -61,7 +66,7 @@
     loads = [
         pltpu.make_async_copy(src, dst, load_sem.at[i])
         for i, (src, dst) in enumerate(
-            ((coef_any, coef_ref), (b_any, b_ref), (p_any, p_ref), (m_any, m_ref), (f_any, f_ref))
+            ((coef_any, coef_ref), (b_any, spaced(b_ref)), (p_any, p_ref), (m_any, m_ref), (f_any, f_ref))
         )
     ]
     for c in loads:
@@ -94,7 +99,7 @@
         for yp in range(2):
             for y in range(4):
                 row = x * 8 + 2 * y + yp
-                stage[0:Q, y * L : y * L + L] = b_ref[pl.ds(row, Q, 32), :]
+                stage[0:Q, y * L : y * L + L] = b_ref[pl.ds(row, Q, PITCH), :]
                 stage[Q : Q + 1, y * L : y * L + L] = coefs[0, pl.ds(row, 1), :]
                 stage[Q + 1 : Q + 2, y * L : y * L + L] = coefs[1, pl.ds(row, 1), :]
             ordered = jnp.dot(stage[...].astype(BF16), perm[...], preferred_element_type=F32)
@@ -500,7 +505,7 @@
         c.start()
     perm[...] = one_hot((512, 512), lambda r, c: source_of(r) == c)
     outs = ((sol_ref, sol_any), (res_ref, res_any))
-    stores = [pltpu.make_async_copy(src, dst, out_sem.at[w]) for w, (src, dst) in enumerate(outs)]
+    stores = [pltpu.make_async_copy(spaced(src), dst, out_sem.at[w]) for w, (src, dst) in enumerate(outs)]
     for w, (out_ref, _) in enumerate(outs):
         loads[w].wait()
 
@@ -511,7 +516,7 @@
             back = jnp.dot(tiles, perm[...], preferred_element_type=F32)
             for yp in range(2):
                 for y in range(4):
-                    out_ref[pl.ds(x * 8 + 2 * y + yp, Q, 32), :] = back[yp * B : yp * B + Q, y * L : y * L + L]
+                    out_ref[pl.ds(x * 8 + 2 * y + yp, Q, PITCH), :] = back[yp * B : yp * B + Q, y * L : y * L + L]
             return carry
 
         lax.fori_loop(0, 4, one, 0)
@@ -521,7 +526,7 @@
 
 
 def on_device(nx, nz, right_side, cell_coef, cell_matrix, face_coupling, patch_inverse):
-    flat = right_side.reshape(-1, L)
+    flat = right_side.reshape(Q, 32, L)
     tile = lambda *dims, t=BF16: pltpu.VMEM((*dims, B if t == BF16 else F, L), t)
     whole = pl.BlockSpec(memory_space=pl.ANY)
     ordered = pl.pallas_call(
@@ -530,7 +535,7 @@
         in_specs=[whole] * 5,
         out_specs=whole,
         scratch_shapes=[
-            pltpu.VMEM(flat.shape, F32),
+            pltpu.VMEM((Q * PITCH, L), F32),
             pltpu.VMEM((32, 32), F32),
             pltpu.VMEM((8 * Q, 8 * Q), BF16),
             pltpu.VMEM((Q, Q), F32),
@@ -580,7 +585,7 @@
         out_specs=[whole] * 2,
         scratch_shapes=[
             tile(2, 4, 4, 2),
-            *[pltpu.VMEM(flat.shape, F32)] * 2,
+            *[pltpu.VMEM((Q * PITCH, L), F32)] * 2,
             pltpu.VMEM((512, 512), BF16),
             pltpu.SemaphoreType.DMA((2,)),
             pltpu.SemaphoreType.DMA((2,)),

time: 102 us -> 100 us (0.980)
  Pallas kernels: 101 us -> 99.4 us
where the time goes in v5:
time: 100 us
  Pallas kernels  99.4 us (99%)
    pallas_call x1, Pallas kernels, on_device(): pl.pallas_call(functools.partial(kernel, nx, nz), out_shape=jax.ShapeDtyp...  94.9 us
    pallas_call x1, Pallas kernels, on_device(): pl.pallas_call(finish, out_shape=[jax.ShapeDtypeStruct(flat.shape, F32)]...  4.5 us

profile of v5, /device:TPU:1, one launch (start us, length us, event | category | flops | bytes accessed | tf_op | source)
XLA Modules:
  0.0 100.0 jit_solution(16273201461905055566)
XLA Ops:
  0.6 94.9 %shard_map.68.in_any = bf16[2,4,4,2,96,128]{5,4,3,2,1,0:T(8,128)(2,1)} custom-call(f32[81,32,128]{2,1,0:T(8,128)} %bitcast.4, f32[32,32]{1,0:T(8,128)} %bitcast.5, bf16[648,648]{1,0:T(8,128)(2,1)} %p_any.1, f32[81,81]{1,0:T(8,128)} %m_any.1, f32[3,81,81]{2,1,0:T(8,128)} %f_any.1), custom_call_target="tpu_custom_call" | custom-call | tf_op jit(solution)/shard_map/pallas_call | solution.py:532
  95.5 4.5 %shard_map.69 = (f32[81,32,128]{2,1,0:T(8,128)}, f32[81,32,128]{2,1,0:T(8,128)}) custom-call(bf16[2,4,4,2,96,128]{5,4,3,2,1,0:T(8,128)(2,1)} %shard_map.68.in_any), custom_call_target="tpu_custom_call" | custom-call | tf_op jit(solution)/shard_map/pallas_call | solution.py:581

commit v6 on v5

--- a/solution.py
+++ b/solution.py
@@ -253,6 +253,8 @@
                 XK[k * B : k * B + B, 2 * L : 3 * L] = roll(edge, 16 * ry - (2 * dx + yp)).astype(BF16)
         width = 256 if g else 384
         OUT[:, :width] = jnp.dot(PINV[...], XK[:, :width], preferred_element_type=F32)
+        if (b, g) != (0, 0):
+            settle(h, a, 1 - g)
         up, down = jnp.zeros((F, L), F32), jnp.zeros((F, L), F32)
         for X, side in ((0, 0), (1, 1), (0, 1), (1, 0)):
             for k, dx, yp, zp, ry, rz in frames(b, g):
@@ -333,6 +335,8 @@
             x_copy(h, g, a, way).wait_recv()
             for yp in range(2):
                 subtract(h, slot(3 - l, a), yp, weights, [pair(ghost, h, g, yp)])
+
+    def settle(h, a, g):
         for c in (x_copy(h, g, a, 0), x_copy(h, g, a, 1)) + (z_copies(h) if g else ()):
             c.wait_send()
 
@@ -465,6 +469,8 @@
             @pl.when(a == 1)
             def _():
                 leave(1, h, R)
+
+            settle(h, a, 1)
 
         each(end)
 

time: 100 us -> 103 us (1.030)
  Pallas kernels: 99.4 us -> 102 us
    pallas_call x1, Pallas kernels: 94.9 us -> 97.7 us  [on_device(): pl.pallas_call(functools.partial(kernel, nx, nz), out_shape=jax.ShapeDtyp...]
where the time goes in v6:
time: 103 us
  Pallas kernels  102 us (99%)
    pallas_call x1, Pallas kernels, on_device(): pl.pallas_call(functools.partial(kernel, nx, nz), out_shape=jax.ShapeDtyp...  97.7 us
    pallas_call x1, Pallas kernels, on_device(): pl.pallas_call(finish, out_shape=[jax.ShapeDtypeStruct(flat.shape, F32)]...  4.5 us

profile of v6, /device:TPU:1, one launch (start us, length us, event | category | flops | bytes accessed | tf_op | source)
XLA Modules:
  0.0 102.8 jit_solution(6858330848091811487)
XLA Ops:
  0.6 97.7 %shard_map.68.in_any = bf16[2,4,4,2,96,128]{5,4,3,2,1,0:T(8,128)(2,1)} custom-call(f32[81,32,128]{2,1,0:T(8,128)} %bitcast.4, f32[32,32]{1,0:T(8,128)} %bitcast.5, bf16[648,648]{1,0:T(8,128)(2,1)} %p_any.1, f32[81,81]{1,0:T(8,128)} %m_any.1, f32[3,81,81]{2,1,0:T(8,128)} %f_any.1), custom_call_target="tpu_custom_call" | custom-call | tf_op jit(solution)/shard_map/pallas_call | solution.py:538
  98.3 4.5 %shard_map.69 = (f32[81,32,128]{2,1,0:T(8,128)}, f32[81,32,128]{2,1,0:T(8,128)}) custom-call(bf16[2,4,4,2,96,128]{5,4,3,2,1,0:T(8,128)(2,1)} %shard_map.68.in_any), custom_call_target="tpu_custom_call" | custom-call | tf_op jit(solution)/shard_map/pallas_call | solution.py:587
